TPU v7x, 32 devices: a whole 2x2x4 slice. The times are simulated.
32 devices in a mesh: table: 16 (over z, y, x), dp: 2 (over core).
Axes of the slice: x: 2, y: 2, z: 4, core: 2. Of those that a mesh axis runs over, the one named last changes fastest.
Arguments:
- tables: bfloat16 [4, 65536, 128], P(None, 'table'), may hold values from -6 to 6
- owner_ids: int32 [32, 4, 256, 1], P(('table', 'dp')), may hold values from 0 to 15; in each aligned block of 256 rows (0 to 255, 256 to 511, ..., all dimensions but the last counted through in order) at most 32 rows name the same one
- row_ids: int32 [32, 4, 256], P(('table', 'dp')), may hold values from 0 to 4095
- session_of: int32 [32, 256], P(('table', 'dp')), may hold values from 0 to 1, never falling along the last dimension, each value on 1 to 200 neighbouring positions
- relevance: float32 [32, 256], P(('table', 'dp')), may hold values from 0.1 to 10
- logit_bias: float32 [32, 256], P(('table', 'dp')), may hold values from -400 to 400
- w_hidden: float32 [512, 512], replicated, may hold values from -0.25 to 0.25
- bias_hidden: float32 [512], replicated, may hold values from -3 to 3
- w_score: float32 [512], replicated, may hold values from -0.9 to 0.9
Outputs:
- emb_step: float32 [4, 65536, 128], P(None, ('table', 'dp'))
- step_hidden: float32 [512, 512], replicated
- step_bias: float32 [512], replicated
- step_score: float32 [512], replicated
- loss: float32 [], replicated
Inputs may be any that keep to these rules, and one draw needn't show every extreme that they name: `owner_ids`: among one device's impressions, for one table, at most 32 name the same owner. `session_of`: session numbers never fall along a device's impressions; each of a device's 2 sessions has 1 to 200 impressions.
All inputs are finite; a program needn't handle non-finite values.
Results may differ from a plain program's by a relative error of at most 0.001.
The roundings to bfloat16 on the way count: a program that leaves them out, or rounds other values in their place, can miss the bound.
Values may be sent and summed in bfloat16 or wider, within the bound.
A program may use at most 64 MiB of HBM per device.

v0:
```python
import jax
import jax.numpy as jnp
from jax import lax
from jax.experimental import pallas as pl
from jax.experimental.pallas import tpu as pltpu
import functools
from jax.sharding import PartitionSpec as P

SESS_DEV = 2


def silu_slope(pre_val):
    logistic = jax.nn.sigmoid(pre_val)
    return logistic * (1.0 + pre_val * (1.0 - logistic))


def session_terms(scores, session_ids, relevance, sessions):
    member = session_ids[None, :] == jnp.arange(sessions, dtype=jnp.int32)[:, None]
    highest = jnp.max(jnp.where(member, scores[None, :], -jnp.inf), axis=1)
    highest_each = jnp.sum(jnp.where(member, highest[:, None], 0.0), axis=0)
    shifted = scores - highest_each
    exponent = jnp.exp(shifted)
    totals = jnp.sum(jnp.where(member, exponent[None, :], 0.0), axis=1)
    weights = jnp.sum(jnp.where(member, relevance[None, :], 0.0), axis=1)
    total_each = jnp.sum(jnp.where(member, totals[:, None], 0.0), axis=0)
    weight_each = jnp.sum(jnp.where(member, weights[:, None], 0.0), axis=0)
    probability = exponent / total_each
    target = relevance / weight_each
    loss_sum = jnp.sum(jnp.log(totals)) - jnp.sum(target * shifted)
    return (loss_sum, probability - target)


def selector(indices, count):
    return (indices[:, None] == jnp.arange(count, dtype=jnp.int32)[None, :]).astype(jnp.bfloat16)


def pick_rows(indices, source):
    return jnp.dot(
        selector(indices, source.shape[0]), source, preferred_element_type=jnp.float32
    ).astype(jnp.bfloat16)


def place_rows(indices, values, count):
    return lax.dot_general(
        selector(indices, count),
        values,
        (((0,), (0,)), ((), ())),
        preferred_element_type=jnp.float32,
    )


def on_device(
    tables, owner_ids, row_ids, session_of, relevance, logit_bias, w_hidden, bias_hidden, w_score
):
    owners = lax.axis_size("table")
    devices = owners * lax.axis_size("dp")
    table_count, shard_rows, emb_width = tables.shape
    owner_now = owner_ids[0, :, :, 0]
    rows_now = row_ids[0]
    imp_count = owner_now.shape[1]
    capacity = 2 * imp_count // owners
    slot_total = owners * capacity
    one_hot = (owner_now[:, :, None] == jnp.arange(owners, dtype=jnp.int32)).astype(jnp.float32)
    places = jnp.arange(imp_count, dtype=jnp.int32)
    lower_tri = (places[:, None] >= places[None, :]).astype(jnp.float32)
    running = jnp.einsum("ij,tjo->tio", lower_tri, one_hot, precision=lax.Precision.HIGHEST)
    rank_in = (jnp.sum(running * one_hot, axis=2) - 1.0).astype(jnp.int32)
    slot_of = owner_now * capacity + rank_in
    slot_hot = (slot_of[:, :, None] == jnp.arange(slot_total, dtype=jnp.int32)).astype(jnp.int32)
    wanted = jnp.sum(slot_hot * rows_now[:, :, None], axis=1) + shard_rows * (
        1 - jnp.sum(slot_hot, axis=1)
    )
    if (
        capacity % 16 == 0
        and table_count * capacity == 128
        and w_hidden.shape[0] == w_hidden.shape[1]
    ):
        return whole_kernel(
            tables,
            jnp.transpose(wanted.reshape(table_count, owners, capacity), (1, 0, 2)),
            slot_of,
            session_of[0],
            relevance[0],
            logit_bias[0],
            w_hidden,
            bias_hidden,
            w_score,
        )
    requested = lax.all_to_all(
        wanted.reshape(table_count, owners, capacity),
        "table",
        split_axis=1,
        concat_axis=1,
        tiled=True,
    )
    served = lax.map(
        lambda pair: pick_rows(pair[0], pair[1]),
        (requested.reshape(table_count, slot_total), tables),
    )
    served = served.reshape(table_count, owners, capacity, emb_width)
    hidden_bf = w_hidden.astype(jnp.bfloat16)
    returned = lax.all_to_all(served, "table", split_axis=1, concat_axis=1, tiled=True).reshape(
        table_count, slot_total, emb_width
    )
    gathered = lax.map(lambda pair: pick_rows(pair[0], pair[1]), (slot_of, returned))
    inputs = jnp.transpose(gathered, (1, 0, 2)).reshape(imp_count, table_count * emb_width)
    pre_act = jnp.dot(inputs, hidden_bf, preferred_element_type=jnp.float32)
    pre_act = pre_act + bias_hidden
    hidden = jax.nn.silu(pre_act)
    scores = jnp.dot(hidden, w_score, precision=lax.Precision.HIGHEST) + logit_bias[0]
    loss_sum, score_grad = session_terms(scores, session_of[0], relevance[0], SESS_DEV)
    pre_grad = score_grad[:, None] * w_score[None, :] * silu_slope(pre_act)
    pre_grad_bf = pre_grad.astype(jnp.bfloat16)
    weight_grad = lax.dot_general(
        inputs, pre_grad_bf, (((0,), (0,)), ((), ())), preferred_element_type=jnp.float32
    )
    bias_grad = jnp.sum(pre_grad, axis=0)
    score_weight_grad = jnp.dot(score_grad, hidden, precision=lax.Precision.HIGHEST)
    input_grad = jnp.dot(pre_grad_bf, hidden_bf.T, preferred_element_type=jnp.float32).astype(
        jnp.bfloat16
    )
    input_grad = jnp.transpose(input_grad.reshape(imp_count, table_count, emb_width), (1, 0, 2))
    outgoing = lax.map(
        lambda pair: place_rows(pair[0], pair[1], slot_total).astype(jnp.bfloat16),
        (slot_of, input_grad),
    )
    incoming = lax.all_to_all(
        outgoing.reshape(table_count, owners, capacity, emb_width),
        "table",
        split_axis=1,
        concat_axis=1,
        tiled=True,
    )
    summed = lax.map(
        lambda pair: place_rows(pair[0], pair[1], shard_rows),
        (
            requested.reshape(table_count, slot_total),
            incoming.reshape(table_count, slot_total, emb_width),
        ),
    )
    own_rows = lax.psum_scatter(summed, "dp", scatter_dimension=1, tiled=True)
    emb_step = own_rows / (jnp.sqrt(jnp.mean(own_rows * own_rows, axis=2, keepdims=True)) + 1e-06)
    param_count = w_hidden.size + bias_hidden.size + w_score.size
    weight_tot, bias_tot, score_tot, loss_tot = lax.psum(
        (weight_grad, bias_grad, score_weight_grad, loss_sum), ("table", "dp")
    )
    mean_sq = (
        jnp.sum(weight_tot * weight_tot)
        + jnp.sum(bias_tot * bias_tot)
        + jnp.sum(score_tot * score_tot)
    ) / param_count
    factor = 1.0 / jnp.sqrt(mean_sq + 1e-06)
    step_hidden = weight_tot * factor
    loss = loss_tot / (SESS_DEV * devices)
    return (emb_step, step_hidden, bias_tot * factor, score_tot * factor, loss)


MESH = pl.DeviceIdType.MESH


def whole_body(
    sizes, tables_hbm, wanted_ref, slots_ref, columns_ref, weights_ref, bias_ref, scorer_ref,
    emb_ref, step_ref, small_ref,
    tables_ref, ids_in, ids_ref, served, picked, picked_rows, gathered, dense_ref, out_ref,
    load_sem, want_sems, want_own, serve_send, serve_recv, serve_own, grads, swapped, ids_other, emb_rows, from_other, from_plane, from_column, sum_pair, sum_plane,
    total, grad_send, grad_recv, own_sem, swap_send, swap_recv, ids_sems, pair_sems, plane_send,
    plane_recv, column_send, column_recv, emb_sem,
):
    tables, owners, capacity, width, half_rows, inner, outer, hid, sessions, own_sessions = sizes
    slots = owners * capacity
    me = lax.axis_index("table")
    core = lax.axis_index("dp")
    low, high = lax.rem(me, inner), me // inner
    other = (me, 1 - core)

    def load(table):
        return pltpu.make_async_copy(
            tables_hbm.at[table], tables_ref.at[table], load_sem.at[table]
        )

    for table in range(tables):
        load(table).start()
    barrier = pltpu.get_barrier_semaphore()

    def greet(step, carry):
        pl.semaphore_signal(
            barrier, inc=1, device_id=(lax.rem(me + step, owners), core), device_id_type=MESH
        )
        return carry

    pl.semaphore_signal(barrier, inc=1, device_id=other, device_id_type=MESH)
    lax.fori_loop(1, owners, greet, 0)
    pl.semaphore_wait(barrier, owners)

    def remote(src, dst, send, recv, to):
        return pltpu.make_async_remote_copy(
            src_ref=src, dst_ref=dst, send_sem=send, recv_sem=recv, device_id=to,
            device_id_type=MESH,
        )

    def to_peers(copy_to):
        def one(step, carry):
            copy_to(lax.rem(me + step, owners)).start()
            return carry

        lax.fori_loop(1, owners, one, 0)

    to_peers(
        lambda peer: remote(
            wanted_ref.at[peer], ids_in.at[me], want_sems.at[0], want_sems.at[1], (peer, core)
        )
    )
    want_mine = pltpu.make_async_copy(wanted_ref.at[me], ids_in.at[me], want_own.at[0])
    want_mine.start()
    w_bf = weights_ref[...].astype(jnp.bfloat16)
    want_mine.wait()
    remote(
        wanted_ref.at[pl.ds(0, owners - 1)], ids_in.at[pl.ds(0, owners - 1)], want_sems.at[0],
        want_sems.at[1], other,
    ).wait()

    depth = 1024
    shard_rows = 2 * half_rows

    def serve_own_copy(table):
        return pltpu.make_async_copy(
            served.at[table, me], picked.at[table, me], serve_own.at[table]
        )

    for table in range(tables):
        named = jnp.broadcast_to(
            ids_in[:, 0:1, :].astype(jnp.float32), (owners, capacity, 128)
        )
        lane = lax.broadcasted_iota(jnp.int32, named.shape, 2)
        place_in = lax.broadcasted_iota(jnp.int32, named.shape, 1) + table * capacity
        wide_ids = jnp.broadcast_to(
            jnp.sum(jnp.where(lane == place_in, named, 0.0), axis=2, keepdims=True), named.shape
        ).reshape(slots, 128).astype(jnp.int32)
        ids_ref[pl.ds(table, 1), :] = wide_ids.T[0:1, :]
        ids_col = wide_ids[:, 0:1]
        load(table).wait()
        picked_rows[...] = jnp.zeros_like(picked_rows)

        def pick_block(step, carry):
            at = lax.broadcasted_iota(jnp.int32, (slots, depth), 1)
            hot = jnp.where(at == ids_col - step * depth, 1.0, 0.0).astype(jnp.bfloat16)
            rows_at = pl.ds(pl.multiple_of(step * depth, depth), depth)
            picked_rows[...] += jnp.dot(
                hot, tables_ref[table, rows_at, :], preferred_element_type=jnp.float32
            )
            return carry

        lax.fori_loop(0, shard_rows // depth, pick_block, 0)
        served[table] = picked_rows[...].astype(jnp.bfloat16).reshape(owners, capacity, width)
        serve_own_copy(table).start()
        to_peers(
            lambda peer, table=table: remote(
                served.at[table, peer], picked.at[table, me], serve_send.at[table],
                serve_recv.at[table], (peer, core),
            )
        )
    ids_copy = remote(ids_ref, ids_other, ids_sems.at[0], ids_sems.at[1], other)
    ids_copy.start()

    imps = gathered.shape[0]
    for table in range(tables):
        serve_own_copy(table).wait()
        remote(
            served.at[table, pl.ds(0, owners - 1)], picked.at[table, pl.ds(0, owners - 1)],
            serve_send.at[table], serve_recv.at[table], other,
        ).wait()
        slot_col = columns_ref[:, table : table + 1].astype(jnp.int32)
        hot = jnp.where(
            lax.broadcasted_iota(jnp.int32, (imps, slots), 1) == slot_col, 1.0, 0.0
        ).astype(jnp.bfloat16)
        gathered[:, table * width : (table + 1) * width] = jnp.dot(
            hot, picked[table].reshape(slots, width), preferred_element_type=jnp.float32
        ).astype(jnp.bfloat16)
    inputs = gathered[...]
    pre_act = jnp.dot(inputs, w_bf, preferred_element_type=jnp.float32) + bias_ref[...]
    logistic = 1.0 / (1.0 + jnp.exp(-pre_act))
    hidden = pre_act * logistic
    session = columns_ref[:, tables : tables + 1].astype(jnp.int32)
    relevance = columns_ref[:, tables + 1 : tables + 2]
    scores = jnp.sum(hidden * scorer_ref[...], axis=1, keepdims=True)
    scores = scores + columns_ref[:, tables + 2 : tables + 3]
    member = lax.broadcasted_iota(jnp.int32, (imps, 128), 1) == session
    highest = jnp.max(jnp.where(member, scores, -jnp.inf), axis=0, keepdims=True)
    highest_each = jnp.sum(jnp.where(member, highest, 0.0), axis=1, keepdims=True)
    shifted = scores - highest_each
    exponent = jnp.exp(shifted)
    totals = jnp.sum(jnp.where(member, exponent, 0.0), axis=0, keepdims=True)
    weights = jnp.sum(jnp.where(member, relevance, 0.0), axis=0, keepdims=True)
    total_each = jnp.sum(jnp.where(member, totals, 0.0), axis=1, keepdims=True)
    weight_each = jnp.sum(jnp.where(member, weights, 0.0), axis=1, keepdims=True)
    target = relevance / weight_each
    real = lax.broadcasted_iota(jnp.int32, (1, 128), 1) < own_sessions
    loss_sum = jnp.sum(jnp.log(jnp.where(real, totals, 1.0)), keepdims=True) - jnp.sum(
        target * shifted, keepdims=True
    )
    score_grad = exponent / total_each - target
    pre_grad = score_grad * scorer_ref[...] * (logistic * (1.0 + pre_act * (1.0 - logistic)))
    pre_grad_bf = pre_grad.astype(jnp.bfloat16)
    weight_grad = lax.dot_general(
        inputs, pre_grad_bf, (((0,), (0,)), ((), ())), preferred_element_type=jnp.float32
    )
    bias_grad = jnp.sum(pre_grad, axis=0, keepdims=True)
    score_weight_grad = jnp.sum(score_grad * hidden, axis=0, keepdims=True)
    line = lax.broadcasted_iota(jnp.int32, (128, hid), 0)
    spot = lax.broadcasted_iota(jnp.int32, (128, hid), 1)
    extra = jnp.where(line == 0, bias_grad, 0.0) + jnp.where(line == 1, score_weight_grad, 0.0)
    extra = extra + jnp.where((line == 2) & (spot == 0), loss_sum, 0.0)
    dense_ref[:, :, :, :, :hid] = weight_grad.reshape(dense_ref.shape[:4] + (hid,))
    dense_ref[:, :, :, :, hid:] = extra.T.reshape(dense_ref.shape[:4] + (128,))
    pair_up = remote(dense_ref.at[1 - core], from_other, pair_sems.at[0], pair_sems.at[1], other)
    pair_up.start()
    input_grad = lax.dot_general(
        pre_grad_bf, w_bf, (((1,), (1,)), ((), ())), preferred_element_type=jnp.float32
    ).astype(jnp.bfloat16)

    def fill(table):
        hot = jnp.where(
            lax.broadcasted_iota(jnp.int32, (slots, imps), 0) == slots_ref[pl.ds(table, 1), :],
            1.0, 0.0,
        ).astype(jnp.bfloat16)
        out_ref[table] = jnp.dot(
            hot, input_grad[:, table * width : (table + 1) * width],
            preferred_element_type=jnp.float32,
        ).astype(jnp.bfloat16).reshape(owners, capacity, width)

    def own_copy(table):
        return pltpu.make_async_copy(
            out_ref.at[table, me], grads.at[table, me], own_sem.at[table]
        )

    def send_grads(table):
        fill(table)
        own_copy(table).start()

        def send_one(step, carry):
            owner = lax.rem(me + step, owners)
            remote(
                out_ref.at[table, owner], grads.at[table, me], grad_send.at[table],
                grad_recv.at[table], (owner, core),
            ).start()
            return carry

        lax.fori_loop(1, owners, send_one, 0)

    def all_grads(table):
        return remote(
            out_ref.at[table, pl.ds(0, owners - 1)], grads.at[table, pl.ds(0, owners - 1)],
            grad_send.at[table], grad_recv.at[table], other,
        )

    def swap(table):
        return remote(
            grads.at[table], swapped.at[table], swap_send.at[table], swap_recv.at[table], other
        )

    def arrive(table):
        own_copy(table).wait()
        all_grads(table).wait()
        swap(table).start()

    block = 256

    def emb_copy(table):
        return pltpu.make_async_copy(emb_rows.at[table], emb_ref.at[table], emb_sem.at[table])

    def place(table):
        swap(table).wait()
        ids_mine = ids_ref[pl.ds(table, 1), :]
        ids_theirs = ids_other[pl.ds(table, 1), :]
        rows_mine = grads[table].reshape(slots, width)
        rows_theirs = swapped[table].reshape(slots, width)

        def place_block(step, carry):
            at = lax.broadcasted_iota(jnp.int32, (block, slots), 0) + (
                core * half_rows + step * block
            )
            hot_mine = jnp.where(at == ids_mine, 1.0, 0.0).astype(jnp.bfloat16)
            hot_theirs = jnp.where(at == ids_theirs, 1.0, 0.0).astype(jnp.bfloat16)
            summed = jnp.dot(hot_mine, rows_mine, preferred_element_type=jnp.float32)
            summed = summed + jnp.dot(hot_theirs, rows_theirs, preferred_element_type=jnp.float32)
            mean = jnp.sum(summed * summed, axis=1, keepdims=True) / width
            emb_rows[table, pl.ds(pl.multiple_of(step * block, block), block), :] = summed / (
                jnp.sqrt(mean) + 1e-06
            )
            return carry

        lax.fori_loop(0, half_rows // block, place_block, 0)
        emb_copy(table).start()

    def plane_copies(phase, src_of, dst_of):
        return [
            remote(
                src_of(lax.rem(low + step, inner)), dst_of(step - 1), plane_send.at[phase, step - 1],
                plane_recv.at[phase, step - 1], (high * inner + lax.rem(low + step, inner), core),
            )
            for step in range(1, inner)
        ]

    def column_copies(phase, src_of, dst_of):
        return [
            remote(
                src_of(lax.rem(high + step, outer)), dst_of(step - 1), column_send.at[phase, step - 1],
                column_recv.at[phase, step - 1], (lax.rem(high + step, outer) * inner + low, core),
            )
            for step in range(1, outer)
        ]

    def run(copies):
        for copy in copies:
            copy.start()

    def finish(copies):
        for copy in copies:
            copy.wait()

    send_grads(0)
    pair_up.wait()
    sum_pair[...] = dense_ref[core] + from_other[...]
    plane_sum = plane_copies(0, lambda to: sum_pair.at[to], lambda slot: from_plane.at[slot])
    run(plane_sum)
    for table in range(1, tables):
        send_grads(table)
    ids_copy.wait()
    finish(plane_sum)
    part = sum_pair[low]
    for slot in range(inner - 1):
        part = part + from_plane[slot]
    sum_plane[...] = part
    column_sum = column_copies(0, lambda to: sum_plane.at[to], lambda slot: from_column.at[slot])
    run(column_sum)
    arrive(0)
    finish(column_sum)
    part = sum_plane[high]
    for slot in range(outer - 1):
        part = part + from_column[slot]
    total[core, low, high] = part
    column_share = column_copies(
        1, lambda to: total.at[core, low, high], lambda slot: total.at[core, low, high]
    )
    run(column_share)
    place(0)
    for table in range(1, tables):
        if table == 1:
            finish(column_share)
            plane_share = plane_copies(
                1, lambda to: total.at[core, low], lambda slot: total.at[core, low]
            )
            run(plane_share)
        arrive(table)
        if table == tables - 1:
            finish(plane_share)
            pair_down = remote(
                total.at[core], total.at[core], pair_sems.at[2], pair_sems.at[3], other
            )
            pair_down.start()
        place(table)
    pair_down.wait()
    every = total[...].reshape(2 * owners * dense_ref.shape[3], dense_ref.shape[4])
    weights, extra = every[:, :hid], every[:, hid:]
    counted = lax.broadcasted_iota(jnp.int32, extra.shape, 1) < 2
    counts = jnp.where(counted, extra, 0.0)
    squares = jnp.sum(weights * weights, keepdims=True) + jnp.sum(counts * counts, keepdims=True)
    factor = 1.0 / jnp.sqrt(squares / (hid * hid + 2 * hid) + 1e-06)
    step_ref[...] = weights * factor
    scaled = jnp.where(counted, extra * factor, extra / sessions)
    small_ref[...] = scaled.T
    for table in range(tables):
        emb_copy(table).wait()


def whole_kernel(
    tables, wanted, slot_of, session, relevance, logit_bias, w_hidden, bias_hidden, w_score
):
    table_count, shard_rows, width = tables.shape
    owners, _, capacity = wanted.shape
    hid = w_hidden.shape[1]
    imps = session.shape[0]
    slots = owners * capacity
    half_rows = shard_rows // 2
    inner = 1
    while inner * inner < owners:
        inner *= 2
    outer = owners // inner
    rows = hid // (2 * owners)
    wide = hid + 128
    wanted = jnp.broadcast_to(
        wanted.reshape(owners, 1, table_count * capacity), (owners, 8, table_count * capacity)
    )
    columns = jnp.stack(
        [slot_of[table].astype(jnp.float32) for table in range(table_count)]
        + [session.astype(jnp.float32), relevance, logit_bias],
        axis=1,
    )
    sizes = (
        table_count, owners, capacity, width, half_rows, inner, outer, hid,
        SESS_DEV * owners * 2, SESS_DEV,
    )
    f32, bf16 = jnp.float32, jnp.bfloat16
    dma = pltpu.SemaphoreType.DMA
    vmem = pl.BlockSpec(memory_space=pltpu.VMEM)
    emb_step, step_hidden, small = pl.pallas_call(
        functools.partial(whole_body, sizes),
        out_shape=(
            jax.ShapeDtypeStruct((table_count, half_rows, width), f32),
            jax.ShapeDtypeStruct((hid, hid), f32),
            jax.ShapeDtypeStruct((128, hid), f32),
        ),
        in_specs=[pl.BlockSpec(memory_space=pl.ANY)] + [vmem] * 6,
        out_specs=(pl.BlockSpec(memory_space=pl.ANY), vmem, vmem),
        scratch_shapes=[
            pltpu.VMEM(tables.shape, bf16),
            pltpu.VMEM(wanted.shape, jnp.int32),
            pltpu.VMEM((table_count, slots), jnp.int32),
            pltpu.VMEM((table_count, owners, capacity, width), bf16),
            pltpu.VMEM((table_count, owners, capacity, width), bf16),
            pltpu.VMEM((slots, width), f32),
            pltpu.VMEM((imps, table_count * width), bf16),
            pltpu.VMEM((2, inner, outer, rows, wide), f32),
            pltpu.VMEM((table_count, owners, capacity, width), bf16),
            dma((table_count,)), dma((2,)), dma((1,)),
            dma((table_count,)), dma((table_count,)), dma((table_count,)),
            pltpu.VMEM((table_count, owners, capacity, width), bf16),
            pltpu.VMEM((table_count, owners, capacity, width), bf16),
            pltpu.VMEM((table_count, slots), jnp.int32),
            pltpu.VMEM((table_count, half_rows, width), f32),
            pltpu.VMEM((inner, outer, rows, wide), f32),
            pltpu.VMEM((inner - 1, outer, rows, wide), f32),
            pltpu.VMEM((outer - 1, rows, wide), f32),
            pltpu.VMEM((inner, outer, rows, wide), f32),
            pltpu.VMEM((outer, rows, wide), f32),
            pltpu.VMEM((2, inner, outer, rows, wide), f32),
            dma((table_count,)), dma((table_count,)), dma((table_count,)),
            dma((table_count,)), dma((table_count,)),
            dma((2,)), dma((4,)),
            dma((2, inner - 1)), dma((2, inner - 1)), dma((2, outer - 1)), dma((2, outer - 1)),
            dma((table_count,)),
        ],
        compiler_params=pltpu.CompilerParams(
            collective_id=1, has_side_effects=True, vmem_limit_bytes=60 * 1024 * 1024
        ),
    )(tables, wanted, slot_of, columns, w_hidden, bias_hidden[None, :], w_score[None, :])
    return (emb_step, step_hidden, small[0], small[1], small[2, 0])


def solution(mesh):
    in_specs = (
        P(None, "table", None),
        P(("table", "dp"), None, None, None),
        P(("table", "dp"), None, None),
        P(("table", "dp"), None),
        P(("table", "dp"), None),
        P(("table", "dp"), None),
        P(),
        P(),
        P(),
    )
    out_specs = (P(None, ("table", "dp"), None), P(), P(), P(), P())
    return jax.shard_map(
        on_device, mesh=mesh, in_specs=in_specs, out_specs=out_specs, check_vma=False
    )
```

profile of v0, /device:TPU:0, one launch (start us, length us, event | category | flops | bytes accessed | tf_op | source)
XLA Modules:
  0.0 83.3 jit_solution(14216531886805906718)
XLA Ops:
  0.6 0.7 copy.37
  1.3 0.2 fusion.1
  1.5 0.7 convert_add_fusion.slots_ref
  2.2 0.0 copy-start.1
  2.2 0.7 fusion.5
  2.9 0.7 stack.2
  3.6 0.8 copy.32.columns_ref
  4.4 1.2 %convert_reduce_fusion = (s32[4,512]{1,0:T(4,128)S(1)}, s32[4,512]{1,0:T(4,128)S(1)}) fusion(s32[4,256]{1,0:T(4,128)S(1)} %convert_add_fusion.slots_ref, s32[4,256]{1,0:T(4,128)} %bitcast.35), kind=kLoop, calls=%fused_computation | loop fusion | flops 2617344 | bytes 24576 | tf_op jit(solution)/shard_map/reduce_sum | solution.py:71
  5.7 0.1 add.17
  5.8 0.1 broadcast_in_dim.8
  5.9 0.6 broadcast_in_dim.9.wanted_ref
  6.5 0.0 copy-done.1
  6.5 68.6 %shard_map.128 = (f32[4,2048,128]{2,1,0:T(8,128)}, f32[512,512]{1,0:T(8,128)}, f32[128,512]{1,0:T(8,128)}) custom-call(bf16[4,4096,128]{2,1,0:T(8,128)(2,1)} %tables_hbm.1, s32[16,8,128]{2,1,0:T(8,128)} %broadcast_in_dim.9.wanted_ref, s32[4,256]{1,0:T(4,128)} %copy-done.1, f32[256,7]{1,0:T(8,128)} %copy.32.columns_ref, f32[512,512]{1,0:T(8,128)} %weights_ref.1, ...), custom_call_target="tpu_custom_call" | custom-call | tf_op jit(solution)/shard_map/pallas_call | solution.py:506
  75.1 1.4 %fusion.9 = (f32[1,512]{1,0:T(1,128)}, f32[1,512]{1,0:T(1,128)}) fusion(f32[128,512]{1,0:T(8,128)} %get-tuple-element.10), kind=kLoop, calls=%fused_computation.22 | loop fusion | bytes 8192 | tf_op jit(solution)/shard_map/slice | solution.py:547
  76.5 1.2 %slice.27 = f32[1,1]{1,0:T(1,128)} slice(f32[128,512]{1,0:T(8,128)} %get-tuple-element.10), slice={[2:3], [0:1]} | slice | bytes 8 | tf_op jit(solution)/shard_map/slice | solution.py:547
  77.7 0.0 copy-start
  77.7 4.6 %copy.40 = f32[4,2048,128]{2,1,0:T(8,128)} copy(f32[4,2048,128]{2,1,0:T(8,128)} %get-tuple-element.25) | data formatting | bytes 8388608
  82.3 0.0 copy-done
  82.3 1.0 %copy.41 = f32[512,512]{1,0:T(8,128)} copy(f32[512,512]{1,0:T(8,128)S(1)} %copy-done) | data formatting | bytes 2097152
  (2 shorter events, 0.0 us)
Async XLA Ops:
  2.2 4.3 %copy-start.1 = (s32[4,256]{1,0:T(4,128)}, s32[4,256]{1,0:T(4,128)S(1)}, u32[]{:S(2)}) copy-start(s32[4,256]{1,0:T(4,128)S(1)} %convert_add_fusion.slots_ref) | copy-start | bytes 12292
  77.7 4.6 %copy-start = (f32[512,512]{1,0:T(8,128)S(1)}, f32[512,512]{1,0:T(8,128)}, u32[]{:S(2)}) copy-start(f32[512,512]{1,0:T(8,128)} %get-tuple-element.26) | copy-start | bytes 3145732
where the time goes:
time: 83.7 us; the launch traced here: 83.3 us
  Pallas kernels  68.6 us (82%)
  local copies, waits for them, and re-layouts  11.1 us (13%)
  other arithmetic  2.61 us (3%)
    pallas_call x1, Pallas kernels, whole_kernel(): pl.pallas_call(functools.partial(whole_body, sizes), out_shape=(jax.Shape...  68.6 us
    unnamed x7, local copies, waits for them, and re-layouts  6.23 us
    slice x2, local copies, waits for them, and re-layouts, whole_kernel(): return (emb_step, step_hidden, small[0], small[1], small[2, 0])  2.57 us

commit v1 on v0

--- a/solution.py
+++ b/solution.py
@@ -160,11 +160,11 @@
 
 def whole_body(
     sizes, tables_hbm, wanted_ref, slots_ref, columns_ref, weights_ref, bias_ref, scorer_ref,
-    emb_ref, step_ref, small_ref,
+    emb_rows, step_ref, small_ref,
     tables_ref, ids_in, ids_ref, served, picked, picked_rows, gathered, dense_ref, out_ref,
-    load_sem, want_sems, want_own, serve_send, serve_recv, serve_own, grads, swapped, ids_other, emb_rows, from_other, from_plane, from_column, sum_pair, sum_plane,
+    load_sem, want_sems, want_own, serve_send, serve_recv, serve_own, grads, swapped, ids_other, from_other, from_plane, from_column, sum_pair, sum_plane,
     total, grad_send, grad_recv, own_sem, swap_send, swap_recv, ids_sems, pair_sems, plane_send,
-    plane_recv, column_send, column_recv, emb_sem,
+    plane_recv, column_send, column_recv,
 ):
     tables, owners, capacity, width, half_rows, inner, outer, hid, sessions, own_sessions = sizes
     slots = owners * capacity
@@ -365,8 +365,6 @@
 
     block = 256
 
-    def emb_copy(table):
-        return pltpu.make_async_copy(emb_rows.at[table], emb_ref.at[table], emb_sem.at[table])
 
     def place(table):
         swap(table).wait()
@@ -390,7 +388,6 @@
             return carry
 
         lax.fori_loop(0, half_rows // block, place_block, 0)
-        emb_copy(table).start()
 
     def plane_copies(phase, src_of, dst_of):
         return [
@@ -469,8 +466,23 @@
     step_ref[...] = weights * factor
     scaled = jnp.where(counted, extra * factor, extra / sessions)
     small_ref[...] = scaled.T
-    for table in range(tables):
-        emb_copy(table).wait()
+
+
+def write_body(
+    rows_ref, weights_ref, small_ref, emb_ref, hidden_ref, bias_ref, score_ref, loss_ref, sems
+):
+    copies = [
+        pltpu.make_async_copy(rows_ref.at[table], emb_ref.at[table], sems.at[table])
+        for table in range(rows_ref.shape[0])
+    ]
+    for copy in copies:
+        copy.start()
+    hidden_ref[...] = weights_ref[...]
+    bias_ref[...] = small_ref[0:1, :]
+    score_ref[...] = small_ref[1:2, :]
+    loss_ref[...] = small_ref[2:3, 0:1]
+    for copy in copies:
+        copy.wait()
 
 
 def whole_kernel(
@@ -511,7 +523,7 @@
             jax.ShapeDtypeStruct((128, hid), f32),
         ),
         in_specs=[pl.BlockSpec(memory_space=pl.ANY)] + [vmem] * 6,
-        out_specs=(pl.BlockSpec(memory_space=pl.ANY), vmem, vmem),
+        out_specs=(vmem, vmem, vmem),
         scratch_shapes=[
             pltpu.VMEM(tables.shape, bf16),
             pltpu.VMEM(wanted.shape, jnp.int32),
@@ -527,7 +539,6 @@
             pltpu.VMEM((table_count, owners, capacity, width), bf16),
             pltpu.VMEM((table_count, owners, capacity, width), bf16),
             pltpu.VMEM((table_count, slots), jnp.int32),
-            pltpu.VMEM((table_count, half_rows, width), f32),
             pltpu.VMEM((inner, outer, rows, wide), f32),
             pltpu.VMEM((inner - 1, outer, rows, wide), f32),
             pltpu.VMEM((outer - 1, rows, wide), f32),
@@ -538,13 +549,16 @@
             dma((table_count,)), dma((table_count,)),
             dma((2,)), dma((4,)),
             dma((2, inner - 1)), dma((2, inner - 1)), dma((2, outer - 1)), dma((2, outer - 1)),
-            dma((table_count,)),
         ],
         compiler_params=pltpu.CompilerParams(
-            collective_id=1, has_side_effects=True, vmem_limit_bytes=60 * 1024 * 1024
+            collective_id=1, has_side_effects=True, vmem_limit_bytes=36 * 1024 * 1024
         ),
     )(tables, wanted, slot_of, columns, w_hidden, bias_hidden[None, :], w_score[None, :])
-    return (emb_step, step_hidden, small[0], small[1], small[2, 0])
+    emb_step, step_hidden, b, c, d = pl.pallas_call(write_body, out_shape=(jax.ShapeDtypeStruct((table_count, half_rows, width), f32),
+            jax.ShapeDtypeStruct((hid, hid), f32),jax.ShapeDtypeStruct((1, hid), f32),jax.ShapeDtypeStruct((1, hid), f32),jax.ShapeDtypeStruct((1, 1), f32)),
+            in_specs=[vmem]*3, out_specs=(pl.BlockSpec(memory_space=pl.ANY),vmem,vmem,vmem,vmem), scratch_shapes=[dma((table_count,))],
+            compiler_params=pltpu.CompilerParams(vmem_limit_bytes=8*1024*1024))(emb_step, step_hidden, small)
+    return (emb_step, step_hidden, b[0], c[0], d[0, 0])
 
 
 def solution(mesh):

time: 83.7 us -> 79.7 us (0.952)
  local copies, waits for them, and re-layouts: 11.1 us -> 6.5 us
    pallas_call x0 -> x1, Pallas kernels: none -> 3.02 us  [whole_kernel(): pl.pallas_call(write_body, out_shape=(jax.ShapeDtypeStruct((table_count,...]
    slice x2 -> x0, local copies, waits for them, and re-layouts: 2.57 us -> none  [whole_kernel(): return (emb_step, step_hidden, small[0], small[1], small[2, 0])]
    pallas_call x1, Pallas kernels: 68.6 us -> 66.3 us  [whole_kernel(): pl.pallas_call(functools.partial(whole_body, sizes), out_shape=(jax.Shape...]
    unnamed x7 -> x9, local copies, waits for them, and re-layouts: 6.23 us -> 5.46 us
where the time goes in v1:
time: 79.7 us; the launch traced here: 79.3 us
  Pallas kernels  69.3 us (87%)
  local copies, waits for them, and re-layouts  6.5 us (8%)
  other arithmetic  2.62 us (3%)
    pallas_call x1, Pallas kernels, whole_kernel(): pl.pallas_call(functools.partial(whole_body, sizes), out_shape=(jax.Shape...  66.3 us
    unnamed x9, local copies, waits for them, and re-layouts  5.46 us
    pallas_call x1, Pallas kernels, whole_kernel(): pl.pallas_call(write_body, out_shape=(jax.ShapeDtypeStruct((table_count,...  3.02 us

profile of v1, /device:TPU:0, one launch (start us, length us, event | category | flops | bytes accessed | tf_op | source)
XLA Modules:
  0.0 79.3 jit_solution(14569086294401680043)
XLA Ops:
  0.6 0.7 copy.37
  1.3 0.2 fusion.1
  1.5 0.7 convert_add_fusion.slots_ref
  2.2 0.7 fusion.5
  2.9 0.7 stack.2
  3.6 1.2 %convert_reduce_fusion = (s32[4,512]{1,0:T(4,128)S(1)}, s32[4,512]{1,0:T(4,128)S(1)}) fusion(s32[4,256]{1,0:T(4,128)S(1)} %convert_add_fusion.slots_ref, s32[4,256]{1,0:T(4,128)} %bitcast.37), kind=kLoop, calls=%fused_computation | loop fusion | flops 2617344 | bytes 24576 | tf_op jit(solution)/shard_map/reduce_sum | solution.py:71
  4.9 0.1 add.17
  5.0 0.1 broadcast_in_dim.8
  5.1 0.1 copy.32.columns_ref
  5.2 0.0 copy-start
  5.2 2.2 %copy-done = bf16[4,4096,128]{2,1,0:T(8,128)(2,1)S(1)} copy-done((bf16[4,4096,128]{2,1,0:T(8,128)(2,1)S(1)}, bf16[4,4096,128]{2,1,0:T(8,128)(2,1)}, u32[]{:S(2)}) %copy-start) | copy-done | bytes 4194328
  7.4 0.0 copy-start.1
  7.4 1.2 %copy-done.1 = f32[512,512]{1,0:T(8,128)S(1)} copy-done((f32[512,512]{1,0:T(8,128)S(1)}, f32[512,512]{1,0:T(8,128)}, u32[]{:S(2)}) %copy-start.1) | copy-done | bytes 1048600
  8.6 0.0 copy-start.2
  8.6 0.7 copy-done.2
  9.3 0.0 copy-start.3
  9.3 0.7 copy-done.3
  10.0 66.3 %shard_map.128 = (f32[4,2048,128]{2,1,0:T(8,128)S(1)}, f32[512,512]{1,0:T(8,128)S(1)}, f32[128,512]{1,0:T(8,128)S(1)}) custom-call(bf16[4,4096,128]{2,1,0:T(8,128)(2,1)S(1)} %copy-done, s32[16,8,128]{2,1,0:T(8,128)S(1)} %broadcast_in_dim.9.wanted_ref, s32[4,256]{1,0:T(4,128)S(1)} %convert_add_fusion.slots_ref, f32[256,7]{1,0:T(8,128)S(1)} %copy.32.columns_ref, ...), custom_call_target="tpu_custom_call" | custom-call | tf_op jit(solution)/shard_map/pallas_call | solution.py:518
  76.3 3.0 %shard_map.129 = (f32[4,2048,128]{2,1,0:T(8,128)}, f32[512,512]{1,0:T(8,128)}, f32[1,512]{1,0:T(1,128)}, f32[1,512]{1,0:T(1,128)}, f32[1,1]{1,0:T(1,128)}) custom-call(f32[4,2048,128]{2,1,0:T(8,128)S(1)} %get-tuple-element.13.rows_ref, f32[512,512]{1,0:T(8,128)S(1)} %get-tuple-element.14.weights_ref, f32[128,512]{1,0:T(8,128)S(1)} %get-tuple-element.15.small_ref), custom_call_target="tpu_custom_call" | custom-call | tf_op jit(solution)/shard_map/pallas_call | solution.py:557
  (3 shorter events, 0.0 us)
Async XLA Ops:
  5.2 2.2 %copy-start = (bf16[4,4096,128]{2,1,0:T(8,128)(2,1)S(1)}, bf16[4,4096,128]{2,1,0:T(8,128)(2,1)}, u32[]{:S(2)}) copy-start(bf16[4,4096,128]{2,1,0:T(8,128)(2,1)} %tables_hbm.1) | copy-start | bytes 12582916
  7.4 1.2 %copy-start.1 = (f32[512,512]{1,0:T(8,128)S(1)}, f32[512,512]{1,0:T(8,128)}, u32[]{:S(2)}) copy-start(f32[512,512]{1,0:T(8,128)} %weights_ref.1) | copy-start | bytes 3145732
  8.6 0.7 copy-start.2
  9.3 0.7 copy-start.3

commit v2 on v1

v2 whole, which is shorter than its diff:
```python
import jax
import jax.numpy as jnp
from jax import lax
from jax.experimental import pallas as pl
from jax.experimental.pallas import tpu as pltpu
import functools
from jax.sharding import PartitionSpec as P

SESS_DEV = 2


def silu_slope(pre_val):
    logistic = jax.nn.sigmoid(pre_val)
    return logistic * (1.0 + pre_val * (1.0 - logistic))


def session_terms(scores, session_ids, relevance, sessions):
    member = session_ids[None, :] == jnp.arange(sessions, dtype=jnp.int32)[:, None]
    highest = jnp.max(jnp.where(member, scores[None, :], -jnp.inf), axis=1)
    highest_each = jnp.sum(jnp.where(member, highest[:, None], 0.0), axis=0)
    shifted = scores - highest_each
    exponent = jnp.exp(shifted)
    totals = jnp.sum(jnp.where(member, exponent[None, :], 0.0), axis=1)
    weights = jnp.sum(jnp.where(member, relevance[None, :], 0.0), axis=1)
    total_each = jnp.sum(jnp.where(member, totals[:, None], 0.0), axis=0)
    weight_each = jnp.sum(jnp.where(member, weights[:, None], 0.0), axis=0)
    probability = exponent / total_each
    target = relevance / weight_each
    loss_sum = jnp.sum(jnp.log(totals)) - jnp.sum(target * shifted)
    return (loss_sum, probability - target)


def selector(indices, count):
    return (indices[:, None] == jnp.arange(count, dtype=jnp.int32)[None, :]).astype(jnp.bfloat16)


def pick_rows(indices, source):
    return jnp.dot(
        selector(indices, source.shape[0]), source, preferred_element_type=jnp.float32
    ).astype(jnp.bfloat16)


def place_rows(indices, values, count):
    return lax.dot_general(
        selector(indices, count),
        values,
        (((0,), (0,)), ((), ())),
        preferred_element_type=jnp.float32,
    )


def on_device(
    tables, owner_ids, row_ids, session_of, relevance, logit_bias, w_hidden, bias_hidden, w_score
):
    owners = lax.axis_size("table")
    devices = owners * lax.axis_size("dp")
    table_count, shard_rows, emb_width = tables.shape
    imp_count = row_ids.shape[2]
    capacity = 2 * imp_count // owners
    if (
        capacity % 16 == 0
        and table_count * capacity == 128
        and w_hidden.shape[0] == w_hidden.shape[1] == table_count * emb_width
        and emb_width == 128
    ):
        return whole_kernel(
            tables,
            owner_ids.reshape(table_count, 1, imp_count),
            row_ids[0],
            session_of,
            relevance,
            logit_bias,
            w_hidden,
            bias_hidden[None, :],
            w_score[None, :],
        )
    owner_now = owner_ids[0, :, :, 0]
    rows_now = row_ids[0]
    slot_total = owners * capacity
    one_hot = (owner_now[:, :, None] == jnp.arange(owners, dtype=jnp.int32)).astype(jnp.float32)
    places = jnp.arange(imp_count, dtype=jnp.int32)
    lower_tri = (places[:, None] >= places[None, :]).astype(jnp.float32)
    running = jnp.einsum("ij,tjo->tio", lower_tri, one_hot, precision=lax.Precision.HIGHEST)
    rank_in = (jnp.sum(running * one_hot, axis=2) - 1.0).astype(jnp.int32)
    slot_of = owner_now * capacity + rank_in
    slot_hot = (slot_of[:, :, None] == jnp.arange(slot_total, dtype=jnp.int32)).astype(jnp.int32)
    wanted = jnp.sum(slot_hot * rows_now[:, :, None], axis=1) + shard_rows * (
        1 - jnp.sum(slot_hot, axis=1)
    )
    requested = lax.all_to_all(
        wanted.reshape(table_count, owners, capacity),
        "table",
        split_axis=1,
        concat_axis=1,
        tiled=True,
    )
    served = lax.map(
        lambda pair: pick_rows(pair[0], pair[1]),
        (requested.reshape(table_count, slot_total), tables),
    )
    served = served.reshape(table_count, owners, capacity, emb_width)
    hidden_bf = w_hidden.astype(jnp.bfloat16)
    returned = lax.all_to_all(served, "table", split_axis=1, concat_axis=1, tiled=True).reshape(
        table_count, slot_total, emb_width
    )
    gathered = lax.map(lambda pair: pick_rows(pair[0], pair[1]), (slot_of, returned))
    inputs = jnp.transpose(gathered, (1, 0, 2)).reshape(imp_count, table_count * emb_width)
    pre_act = jnp.dot(inputs, hidden_bf, preferred_element_type=jnp.float32)
    pre_act = pre_act + bias_hidden
    hidden = jax.nn.silu(pre_act)
    scores = jnp.dot(hidden, w_score, precision=lax.Precision.HIGHEST) + logit_bias[0]
    loss_sum, score_grad = session_terms(scores, session_of[0], relevance[0], SESS_DEV)
    pre_grad = score_grad[:, None] * w_score[None, :] * silu_slope(pre_act)
    pre_grad_bf = pre_grad.astype(jnp.bfloat16)
    weight_grad = lax.dot_general(
        inputs, pre_grad_bf, (((0,), (0,)), ((), ())), preferred_element_type=jnp.float32
    )
    bias_grad = jnp.sum(pre_grad, axis=0)
    score_weight_grad = jnp.dot(score_grad, hidden, precision=lax.Precision.HIGHEST)
    input_grad = jnp.dot(pre_grad_bf, hidden_bf.T, preferred_element_type=jnp.float32).astype(
        jnp.bfloat16
    )
    input_grad = jnp.transpose(input_grad.reshape(imp_count, table_count, emb_width), (1, 0, 2))
    outgoing = lax.map(
        lambda pair: place_rows(pair[0], pair[1], slot_total).astype(jnp.bfloat16),
        (slot_of, input_grad),
    )
    incoming = lax.all_to_all(
        outgoing.reshape(table_count, owners, capacity, emb_width),
        "table",
        split_axis=1,
        concat_axis=1,
        tiled=True,
    )
    summed = lax.map(
        lambda pair: place_rows(pair[0], pair[1], shard_rows),
        (
            requested.reshape(table_count, slot_total),
            incoming.reshape(table_count, slot_total, emb_width),
        ),
    )
    own_rows = lax.psum_scatter(summed, "dp", scatter_dimension=1, tiled=True)
    emb_step = own_rows / (jnp.sqrt(jnp.mean(own_rows * own_rows, axis=2, keepdims=True)) + 1e-06)
    param_count = w_hidden.size + bias_hidden.size + w_score.size
    weight_tot, bias_tot, score_tot, loss_tot = lax.psum(
        (weight_grad, bias_grad, score_weight_grad, loss_sum), ("table", "dp")
    )
    mean_sq = (
        jnp.sum(weight_tot * weight_tot)
        + jnp.sum(bias_tot * bias_tot)
        + jnp.sum(score_tot * score_tot)
    ) / param_count
    factor = 1.0 / jnp.sqrt(mean_sq + 1e-06)
    step_hidden = weight_tot * factor
    loss = loss_tot / (SESS_DEV * devices)
    return (emb_step, step_hidden, bias_tot * factor, score_tot * factor, loss)


MESH = pl.DeviceIdType.MESH
F32, BF16, I16 = jnp.float32, jnp.bfloat16, jnp.int16
CHUNKS = 2
LANES = 128


def iota(shape, dim):
    return lax.broadcasted_iota(jnp.int32, shape, dim)


def ones_where(mask):
    return jnp.where(mask, 1.0, 0.0)


def lane_hits(key, base, blocks):
    at = [(iota((16, LANES), 1) + (base + k * LANES)).astype(I16) for k in range(blocks)]
    one, zero = jnp.ones(key.shape, BF16), jnp.zeros(key.shape, BF16)
    return jnp.concatenate(
        [
            jnp.where(key == jnp.concatenate([lanes] * (key.shape[0] // 16), axis=0), one, zero)
            for lanes in at
        ],
        axis=1,
    )


def whole_body(
    sizes, tables_hbm, owner_hbm, rows_hbm, session_hbm, relevance_hbm, place_hbm, weights_hbm,
    bias_hbm, scorer_hbm,
    emb_rows, share_q, share_s, small_ref,
    tables_ref, owner_ref, asked_rows, session_ref, relevance_ref, place_ref, weights_ref, bias_ref,
    scorer_ref, w_bf, meta_ref, columns_ref, want_ref, ids_in, ids_other, spread_ref, pack_ref,
    ids_cols, place_keys, high_ref, hot_ref, hot_rows, served, picked, gathered, inputs_t, out_ref,
    grads, swapped,
    dense_ref, from_other, sum_pair, plane_q, plane_s, from_plane_q, from_plane_s, sum_plane,
    column_q, column_s, from_column_q, from_column_s,
    extra_ref, extra_other, extra_plane, extra_column, extra_pair, extra_sum,
    load_sem, fetch_sem, want_sems, serve_send, serve_recv, ids_sems, grad_send,
    grad_recv, swap_send, swap_recv, pair_send, pair_recv, plane_send, plane_recv, column_send,
    column_recv, extra_send, extra_recv,
):
    tables, owners, capacity, width, half_rows, inner, outer, hid = sizes
    slots = owners * capacity
    imps = asked_rows.shape[1]
    shard_rows = 2 * half_rows
    me = lax.axis_index("table")
    core = lax.axis_index("dp")
    low, high = lax.rem(me, inner), me // inner
    other = (me, 1 - core)
    half = outer // 2

    barrier = pltpu.get_barrier_semaphore()

    def greet(step, carry):
        pl.semaphore_signal(
            barrier, inc=1, device_id=(lax.rem(me + step, owners), core), device_id_type=MESH
        )
        return carry

    pl.semaphore_signal(barrier, inc=1, device_id=other, device_id_type=MESH)
    lax.fori_loop(1, owners, greet, 0)

    sources = [
        (owner_hbm, owner_ref), (rows_hbm, asked_rows), (session_hbm, session_ref),
        (relevance_hbm, relevance_ref), (place_hbm, place_ref), (weights_hbm, weights_ref),
        (bias_hbm, bias_ref), (scorer_hbm, scorer_ref),
    ]
    fetches = [
        pltpu.make_async_copy(src, dst, fetch_sem.at[at]) for at, (src, dst) in enumerate(sources)
    ]

    def load(table):
        return pltpu.make_async_copy(
            tables_hbm.at[table], tables_ref.at[table], load_sem.at[table]
        )

    for fetch in fetches:
        fetch.start()
    for table in range(tables):
        load(table).start()

    def remote(src, dst, send, recv, to):
        return pltpu.make_async_remote_copy(
            src_ref=src, dst_ref=dst, send_sem=send, recv_sem=recv, device_id=to,
            device_id_type=MESH,
        )

    def to_peers(copy_to):
        def far(step, carry):
            plane = (1 - high // half) * half + step // inner
            copy_to(plane * inner + lax.rem(low + lax.rem(step, inner), inner)).start()
            return carry

        def near(step, carry):
            plane = (high // half) * half + lax.rem(lax.rem(high, half) + 1 + step // inner, half)
            copy_to(plane * inner + lax.rem(low + lax.rem(step, inner), inner)).start()
            return carry

        def level(step, carry):
            copy_to(high * inner + lax.rem(low + step, inner)).start()
            return carry

        lax.fori_loop(0, half * inner, far, 0)
        lax.fori_loop(0, (half - 1) * inner, near, 0)
        lax.fori_loop(1, inner, level, 0)

    for fetch in fetches[:5]:
        fetch.wait()
    asked = [ones_where(iota((owners, imps), 0) == owner_ref[table]) for table in range(tables)]
    upto = ones_where(iota((imps, imps), 0) <= iota((imps, imps), 1)).astype(BF16)
    running = jnp.dot(
        jnp.concatenate(asked, axis=0).astype(BF16), upto, preferred_element_type=F32
    )
    tops, lows, keys = [], [], []
    meta_ref[...] = jnp.zeros_like(meta_ref)
    for table in range(tables):
        rank = jnp.sum(
            asked[table] * running[table * owners : (table + 1) * owners], axis=0, keepdims=True
        ) - 1.0
        meta_ref[table : table + 1, :] = owner_ref[table].astype(F32) * capacity + rank
        code = asked_rows[table : table + 1, :] + 1
        tops.append(asked[table] * (code >> 6).astype(F32))
        lows.append(asked[table] * (code & 63).astype(F32))
        keys.append(
            ones_where(iota((LANES, imps), 0) == rank.astype(jnp.int32) + table * capacity)
        )
    codes = jnp.concatenate(
        [jnp.concatenate(tops, axis=1), jnp.concatenate(lows, axis=1)], axis=0
    ).astype(BF16)
    packed = lax.dot_general(
        codes, jnp.concatenate(keys, axis=1).astype(BF16), (((1,), (1,)), ((), ())),
        preferred_element_type=F32,
    )
    want_ref[...] = (packed[:owners] * 64.0 + packed[owners:]).reshape(owners, 1, LANES)
    with jax.named_scope("barrier_wait"):
        pl.semaphore_wait(barrier, owners)

    to_peers(
        lambda peer: remote(
            want_ref.at[peer], ids_in.at[me], want_sems.at[0], want_sems.at[1], (peer, core)
        )
    )
    ids_in[me] = want_ref[me]

    meta_ref[tables : tables + 1, :] = session_ref[...].astype(F32)
    meta_ref[tables + 1 : tables + 2, :] = relevance_ref[...]
    meta_ref[tables + 2 : tables + 3, :] = place_ref[...]
    columns_ref[...] = meta_ref[...].T
    block_of = lax.rem(iota((2 * LANES, tables * LANES), 0), LANES) // capacity
    scale = jnp.where(iota((2 * LANES, tables * LANES), 0) < LANES, 64.0, 1.0)
    spread_ref[...] = jnp.where(
        block_of == iota((2 * LANES, tables * LANES), 1) // LANES, scale, 0.0
    ).astype(BF16)
    pack_at = iota((8, 2 * LANES), 1)
    pack_ref[...] = jnp.where(
        lax.rem(pack_at, LANES) // capacity == iota((8, 2 * LANES), 0),
        jnp.where(pack_at < LANES, 64.0, 1.0), 0.0,
    ).astype(BF16)
    for fetch in fetches[5:]:
        fetch.wait()
    w_bf[...] = weights_ref[...].astype(BF16)

    def expand(ids):
        got = ids[...]
        top = jnp.floor(got * (1.0 / 64.0))
        shape = (owners, capacity, LANES)
        keep = lax.rem(iota(shape, 2), capacity) == iota(shape, 1)
        parts = [
            jnp.where(keep, jnp.broadcast_to(part, shape), 0.0).astype(BF16).reshape(slots, LANES)
            for part in (top, got - top * 64.0)
        ]
        return jnp.concatenate(parts, axis=1)

    def columns_of(codes):
        return jnp.dot(codes, spread_ref[...], preferred_element_type=F32)

    with jax.named_scope("ids_wait"):
        remote(
            want_ref.at[pl.ds(0, owners - 1)], ids_in.at[pl.ds(0, owners - 1)], want_sems.at[0],
            want_sems.at[1], other,
        ).wait()
    ids_copy = remote(ids_in, ids_other, ids_sems.at[0], ids_sems.at[1], other)
    ids_copy.start()
    codes_mine = expand(ids_in)
    ids_cols[...] = columns_of(codes_mine)

    def pick(table):
        code = ids_cols[:, table * LANES : (table + 1) * LANES]
        upper = code > half_rows
        key = jnp.where(upper, code - (half_rows + 1.0), code - 1.0).astype(jnp.int32).astype(I16)
        both = jnp.zeros((slots, 2 * width), F32)
        depth = 256
        for at in range(0, half_rows, depth):
            rows = jnp.concatenate(
                [
                    tables_ref[table, at : at + depth, :],
                    tables_ref[table, half_rows + at : half_rows + at + depth, :],
                ],
                axis=1,
            )
            both = both + jnp.dot(
                lane_hits(key, at, depth // LANES), rows, preferred_element_type=F32
            )
        served[table] = jnp.where(upper, both[:, width:], both[:, :width]).astype(BF16).reshape(
            owners, capacity, width
        )

    with jax.named_scope("pick"):
        for table in range(tables):
            load(table).wait()
            pick(table)
            picked[table, me] = served[table, me]
            to_peers(
                lambda peer, table=table: remote(
                    served.at[table, peer], picked.at[table, me], serve_send.at[table],
                    serve_recv.at[table], (peer, core),
                )
            )

    with jax.named_scope("prep"):
        for table in range(tables):
            hot_ref[table] = ones_where(
                iota((imps, slots), 1) == columns_ref[:, table : table + 1].astype(jnp.int32)
            ).astype(BF16)
            hot_rows[table] = ones_where(
                iota((slots, imps), 0) == meta_ref[table : table + 1, :].astype(jnp.int32)
            ).astype(BF16)
        quarter = half_rows // 2
        first = (core * half_rows).astype(F32)

        def place_prep(codes, columns, at):
            lanes = lax.dot_general(
                pack_ref[...], codes, (((1,), (1,)), ((), ())), preferred_element_type=F32
            ) - (first + 1.0)
            inside = (lanes >= 0.0) & (lanes < half_rows)
            key = jnp.where(lanes >= quarter, lanes - quarter, lanes)
            key = jnp.where(inside, key, -1.0).astype(jnp.int32)
            for table in range(tables):
                place_keys[table, :, at : at + slots] = jnp.broadcast_to(
                    key[table : table + 1, :], (16, slots)
                ).astype(I16)
                column = columns[:, table * LANES : (table + 1) * LANES]
                high_ref[table, at : at + slots, :] = ones_where(
                    column > first + quarter
                ).astype(BF16)

        place_prep(codes_mine, ids_cols[...], 0)
        ids_copy.wait()
        codes_theirs = expand(ids_other)
        place_prep(codes_theirs, columns_of(codes_theirs), slots)

    pre_act = jnp.broadcast_to(bias_ref[...], (imps, hid))
    for table in range(tables):
        with jax.named_scope(f"rows_wait{table}"):
            remote(
                served.at[table, pl.ds(0, owners - 1)], picked.at[table, pl.ds(0, owners - 1)],
                serve_send.at[table], serve_recv.at[table], other,
            ).wait()
        own = jnp.dot(
            hot_ref[table], picked[table].reshape(slots, width), preferred_element_type=F32
        )
        gathered[:, table * width : (table + 1) * width] = own.astype(BF16)
        inputs_t[table * width : (table + 1) * width, :] = own.T.astype(BF16)
    with jax.named_scope("dense"):
        pre_act = jnp.dot(gathered[...], w_bf[...], preferred_element_type=F32) + bias_ref[...]
        logistic = 1.0 / (1.0 + jnp.exp(-pre_act))
        hidden = pre_act * logistic
        session = columns_ref[:, tables : tables + 1].astype(jnp.int32)
        relevance = columns_ref[:, tables + 1 : tables + 2]
        scores = jnp.sum(hidden * scorer_ref[...], axis=1, keepdims=True)
        scores = scores + columns_ref[:, tables + 2 : tables + 3]
        member = iota((imps, LANES), 1) == session
        highest = jnp.max(jnp.where(member, scores, -jnp.inf), axis=0, keepdims=True)
        highest_each = jnp.sum(jnp.where(member, highest, 0.0), axis=1, keepdims=True)
        shifted = scores - highest_each
        exponent = jnp.exp(shifted)
        sums = jnp.sum(jnp.where(member, exponent, 0.0), axis=0, keepdims=True)
        weights = jnp.sum(jnp.where(member, relevance, 0.0), axis=0, keepdims=True)
        sum_each = jnp.sum(jnp.where(member, sums, 0.0), axis=1, keepdims=True)
        weight_each = jnp.sum(jnp.where(member, weights, 0.0), axis=1, keepdims=True)
        target = relevance / weight_each
        real = iota((1, LANES), 1) < SESS_DEV
        loss_sum = jnp.sum(jnp.log(jnp.where(real, sums, 1.0)), keepdims=True) - jnp.sum(
            target * shifted, keepdims=True
        )
        score_grad = exponent / sum_each - target
        pre_grad = score_grad * scorer_ref[...] * (logistic * (1.0 + pre_act * (1.0 - logistic)))
        pre_grad_bf = pre_grad.astype(BF16)
    piece, rows = hid // CHUNKS, hid // (2 * owners)

    def pair_up(chunk):
        return remote(
            dense_ref.at[chunk, 1 - core], from_other.at[chunk], pair_send.at[0, chunk],
            pair_recv.at[0, chunk], other,
        )

    with jax.named_scope("weight_grad"):
        for chunk in range(CHUNKS):
            dense_ref[chunk] = jnp.dot(
                inputs_t[...], pre_grad_bf[:, chunk * piece : (chunk + 1) * piece],
                preferred_element_type=F32,
            ).reshape(dense_ref.shape[1:])
            pair_up(chunk).start()
        extra_ref[...] = jnp.zeros_like(extra_ref)
        extra_ref[0:1, :] = jnp.sum(pre_grad, axis=0, keepdims=True)
        extra_ref[1:2, :] = jnp.sum(score_grad * hidden, axis=0, keepdims=True)
        extra_ref[2:3, :] = jnp.broadcast_to(loss_sum, (1, hid))
        extra_up = remote(extra_ref, extra_other, extra_send.at[0], extra_recv.at[0], other)
        extra_up.start()
    with jax.named_scope("input_grad"):
        input_grad = lax.dot_general(
            pre_grad_bf, w_bf[...], (((1,), (1,)), ((), ())), preferred_element_type=F32
        ).astype(BF16)

    def send_grads(table):
        out_ref[table] = jnp.dot(
            hot_rows[table], input_grad[:, table * width : (table + 1) * width],
            preferred_element_type=F32,
        ).astype(BF16).reshape(owners, capacity, width)
        grads[table, me] = out_ref[table, me]
        to_peers(
            lambda peer: remote(
                out_ref.at[table, peer], grads.at[table, me], grad_send.at[table],
                grad_recv.at[table], (peer, core),
            )
        )

    def swap(table):
        return remote(
            grads.at[table], swapped.at[table], swap_send.at[table], swap_recv.at[table], other
        )

    def arrive(table):
        remote(
            out_ref.at[table, pl.ds(0, owners - 1)], grads.at[table, pl.ds(0, owners - 1)],
            grad_send.at[table], grad_recv.at[table], other,
        ).wait()
        swap(table).start()

    def place(table):
        swap(table).wait()
        values = jnp.concatenate(
            [grads[table].reshape(slots, width), swapped[table].reshape(slots, width)], axis=0
        )
        upper = values * high_ref[table]
        values = jnp.concatenate([values - upper, upper], axis=1)
        block = 256
        one, zero = jnp.ones((block, LANES), BF16), jnp.zeros((block, LANES), BF16)
        for start in range(0, half_rows // 2, block):
            at = (iota((block, LANES), 0) + start).astype(I16)
            hits = [
                jnp.where(
                    jnp.concatenate(
                        [place_keys[table, :, lane : lane + LANES]] * (block // 16), axis=0
                    ) == at, one, zero,
                )
                for lane in range(0, 2 * slots, LANES)
            ]
            both = jnp.dot(jnp.concatenate(hits, axis=1), values, preferred_element_type=F32)
            for part in range(2):
                summed = both[:, part * width : (part + 1) * width]
                mean = jnp.sum(summed * summed, axis=1, keepdims=True) * (1.0 / width)
                rows_at = part * (half_rows // 2) + start
                emb_rows[table, rows_at : rows_at + block, :] = summed * (
                    1.0 / (jnp.sqrt(mean) + 1e-06)
                )

    def to_plane(src_of, dst_of, send, recv):
        for step in range(1, inner):
            to = lax.rem(low + step, inner)
            remote(src_of(to), dst_of(step - 1), send, recv, (high * inner + to, core)).start()

    def to_column(src_of, dst_of, send, recv):
        for step in range(1, outer):
            to = lax.rem(high + step, outer)
            remote(src_of(to), dst_of(step - 1), send, recv, (to * inner + low, core)).start()

    def await_all(src, dst, send, recv):
        remote(src, dst, send, recv, other).wait()

    def plane_sum(chunk):
        for at, (src, dst) in enumerate(((plane_s, from_plane_s), (plane_q, from_plane_q))):
            to_plane(
                lambda to: src.at[chunk, to], lambda slot: dst.at[chunk, slot],
                plane_send.at[at, chunk], plane_recv.at[at, chunk],
            )

    def plane_summed(chunk):
        for at, (src, dst) in enumerate(((plane_s, from_plane_s), (plane_q, from_plane_q))):
            await_all(
                src.at[chunk, pl.ds(0, inner - 1)], dst.at[chunk], plane_send.at[at, chunk],
                plane_recv.at[at, chunk],
            )

    def column_sum(chunk):
        for at, (src, dst) in enumerate(((column_s, from_column_s), (column_q, from_column_q))):
            to_column(
                lambda to: src.at[chunk, to], lambda slot: dst.at[chunk, slot],
                column_send.at[at, chunk], column_recv.at[at, chunk],
            )

    def column_summed(chunk):
        for at, (src, dst) in enumerate(((column_s, from_column_s), (column_q, from_column_q))):
            await_all(
                src.at[chunk, pl.ds(0, outer - 1)], dst.at[chunk], column_send.at[at, chunk],
                column_recv.at[at, chunk],
            )

    def column_share(chunk):
        for at, part in enumerate((share_s, share_q)):
            mine = part.at[chunk, core, low, high]
            to_column(
                lambda to: mine, lambda slot: mine, column_send.at[2 + at, chunk],
                column_recv.at[2 + at, chunk],
            )

    def column_shared(chunk):
        for at, part in enumerate((share_s, share_q)):
            some = part.at[chunk, core, low, pl.ds(0, outer - 1)]
            await_all(some, some, column_send.at[2 + at, chunk], column_recv.at[2 + at, chunk])

    def plane_share(chunk):
        for at, part in enumerate((share_s, share_q)):
            mine = part.at[chunk, core, low]
            to_plane(
                lambda to: mine, lambda slot: mine, plane_send.at[2 + at, chunk],
                plane_recv.at[2 + at, chunk],
            )

    def plane_shared(chunk):
        for at, part in enumerate((share_s, share_q)):
            some = part.at[chunk, core, pl.ds(0, inner - 1)]
            await_all(some, some, plane_send.at[2 + at, chunk], plane_recv.at[2 + at, chunk])

    def pair_down(chunk):
        return [
            remote(
                part.at[chunk, core], part.at[chunk, core], pair_send.at[phase, chunk],
                pair_recv.at[phase, chunk], other,
            )
            for phase, part in ((1, share_s), (2, share_q))
        ]

    def coded(values):
        most = jnp.max(jnp.abs(values), axis=0, keepdims=True)
        most = jnp.where(most < 1e-34, 0.0, most)
        code = jnp.round(values * jnp.where(most > 0.0, 32767.0 / most, 0.0))
        return code.astype(jnp.int32).astype(I16), most * (1.0 / 32767.0)

    def decoded(code, scale):
        return code.astype(jnp.int32).astype(F32) * scale

    def run(copies):
        for copy in copies:
            copy.start()

    def finish(copies):
        for copy in copies:
            copy.wait()

    def pair_step(chunk):
        pair_up(chunk).wait()
        for to in range(inner):
            values = dense_ref[chunk, core, to] + from_other[chunk, to]
            sum_pair[chunk, to] = values
            code, plane_s[chunk, to] = coded(values.reshape(outer * rows, piece))
            plane_q[chunk, to] = code.reshape(outer, rows, piece)
        plane_sum(chunk)
        if chunk == CHUNKS - 1:
            extra_up.wait()
            extra_pair[...] = extra_ref[...] + extra_other[...]
            extra_plane[low] = extra_ref[...] + extra_other[...]
            to_plane(
                lambda to: extra_pair, lambda slot: extra_plane.at[low], extra_send.at[1],
                extra_recv.at[1],
            )

    def plane_step(chunk):
        plane_summed(chunk)
        part = sum_pair[chunk, low].reshape(outer * rows, piece)
        for slot in range(inner - 1):
            part = part + decoded(
                from_plane_q[chunk, slot].reshape(outer * rows, piece), from_plane_s[chunk, slot]
            )
        for to in range(outer):
            values = part[to * rows : (to + 1) * rows]
            sum_plane[chunk, to] = values
            column_q[chunk, to], column_s[chunk, to] = coded(values)
        column_sum(chunk)
        if chunk == CHUNKS - 1:
            some = extra_plane.at[pl.ds(0, inner - 1)]
            await_all(some, some, extra_send.at[1], extra_recv.at[1])
            part = extra_plane[0]
            for slot in range(1, inner):
                part = part + extra_plane[slot]
            extra_sum[...] = part
            extra_column[high] = part
            to_column(
                lambda to: extra_sum, lambda slot: extra_column.at[high], extra_send.at[2],
                extra_recv.at[2],
            )

    def column_step(chunk):
        column_summed(chunk)
        part = sum_plane[chunk, high]
        for slot in range(outer - 1):
            part = part + decoded(from_column_q[chunk, slot], from_column_s[chunk, slot])
        code, scale = coded(part)
        share_q[chunk, core, low, high] = code
        share_s[chunk, core, low, high] = scale
        column_share(chunk)
        if chunk == CHUNKS - 1:
            some = extra_column.at[pl.ds(0, outer - 1)]
            await_all(some, some, extra_send.at[2], extra_recv.at[2])
            part = extra_column[0]
            for slot in range(1, outer):
                part = part + extra_column[slot]
            small_ref[...] = part

    def share_step(chunk):
        column_shared(chunk)
        plane_share(chunk)

    def down_step(chunk):
        plane_shared(chunk)
        run(pair_down(chunk))

    def last_step(chunk):
        finish(pair_down(chunk))

    steps = {
        "send": send_grads, "pair": pair_step, "plane": plane_step, "column": column_step,
        "share": share_step, "down": down_step, "last": last_step, "arrive": arrive, "place": place,
    }
    for word in ORDER:
        with jax.named_scope(word):
            steps[word[:-1]](int(word[-1]))


ORDER = (
    "send0", "pair0", "pair1", "send1", "send2", "plane0", "send3", "plane1", "arrive0",
    "place0", "column0", "arrive1", "place1", "column1", "arrive2", "share0", "share1",
    "place2", "arrive3", "down0", "down1", "place3", "last0", "last1",
)


def write_body(
    params, sessions, rows_hbm, code_ref, scale_ref, small_ref, emb_hbm, hidden_hbm, bias_hbm,
    score_hbm, loss_hbm, hidden_ref, bias_ref, score_ref, loss_ref, row_sems, sems,
):
    copies = [
        pltpu.make_async_copy(rows_hbm.at[table], emb_hbm.at[table], row_sems.at[table])
        for table in range(rows_hbm.shape[0])
    ]
    for copy in copies:
        copy.start()
    hid = hidden_ref.shape[0]
    piece = code_ref.shape[-1]
    small = small_ref[...]
    counts = jnp.where(iota(small.shape, 0) < 2, small, 0.0)
    squares = jnp.sum(counts * counts, keepdims=True)
    for chunk in range(hid // piece):
        part = code_ref[chunk].astype(jnp.int32).astype(F32) * scale_ref[chunk]
        part = part.reshape(hid, piece)
        hidden_ref[:, chunk * piece : (chunk + 1) * piece] = part
        squares = squares + jnp.sum(part * part, keepdims=True)
    factor = 1.0 / jnp.sqrt(squares / params + 1e-06)
    hidden_ref[...] = hidden_ref[...] * factor
    bias_ref[...] = small[0:1, :] * factor
    score_ref[...] = small[1:2, :] * factor
    loss_ref[...] = small[2:3, 0:1] / sessions
    for at, (src, dst) in enumerate(
        (
            (hidden_ref, hidden_hbm), (bias_ref, bias_hbm), (score_ref, score_hbm),
            (loss_ref, loss_hbm),
        )
    ):
        copies.append(pltpu.make_async_copy(src, dst, sems.at[at]))
        copies[-1].start()
    for copy in copies:
        copy.wait()


def whole_kernel(
    tables, owner_ids, row_ids, session, relevance, logit_bias, w_hidden, bias_hidden, w_score
):
    table_count, shard_rows, width = tables.shape
    owners = lax.axis_size("table")
    imps = row_ids.shape[1]
    capacity = 2 * imps // owners
    hid = w_hidden.shape[1]
    slots = owners * capacity
    half_rows = shard_rows // 2
    inner = 1
    while inner * inner < owners:
        inner *= 2
    outer = owners // inner
    rows = hid // (2 * owners)
    piece = hid // CHUNKS
    sizes = (table_count, owners, capacity, width, half_rows, inner, outer, hid)
    dma = pltpu.SemaphoreType.DMA
    vmem = pl.BlockSpec(memory_space=pltpu.VMEM)
    hbm = pl.BlockSpec(memory_space=pltpu.HBM)
    lookups = (table_count, owners, capacity, width)
    emb_rows, codes, scales, small = pl.pallas_call(
        functools.partial(whole_body, sizes),
        out_shape=(
            jax.ShapeDtypeStruct((table_count, half_rows, width), F32),
            jax.ShapeDtypeStruct((CHUNKS, 2, inner, outer, rows, piece), I16),
            jax.ShapeDtypeStruct((CHUNKS, 2, inner, outer, 1, piece), F32),
            jax.ShapeDtypeStruct((8, hid), F32),
        ),
        in_specs=[hbm] * 9,
        out_specs=(vmem, vmem, vmem, vmem),
        scratch_shapes=[
            pltpu.VMEM(tables.shape, BF16),
            pltpu.VMEM(owner_ids.shape, jnp.int32),
            pltpu.VMEM(row_ids.shape, jnp.int32),
            pltpu.VMEM(session.shape, jnp.int32),
            pltpu.VMEM(relevance.shape, F32),
            pltpu.VMEM(logit_bias.shape, F32),
            pltpu.VMEM(w_hidden.shape, F32),
            pltpu.VMEM(bias_hidden.shape, F32),
            pltpu.VMEM(w_score.shape, F32),
            pltpu.VMEM(w_hidden.shape, BF16),
            pltpu.VMEM((LANES, imps), F32),
            pltpu.VMEM((imps, LANES), F32),
            pltpu.VMEM((owners, 1, LANES), F32),
            pltpu.VMEM((owners, 1, LANES), F32),
            pltpu.VMEM((owners, 1, LANES), F32),
            pltpu.VMEM((2 * LANES, table_count * LANES), BF16),
            pltpu.VMEM((8, 2 * LANES), BF16),
            pltpu.VMEM((slots, table_count * LANES), F32),
            pltpu.VMEM((table_count, 16, 2 * slots), I16),
            pltpu.VMEM((table_count, 2 * slots, LANES), BF16),
            pltpu.VMEM((table_count, imps, slots), BF16),
            pltpu.VMEM((table_count, slots, imps), BF16),
            pltpu.VMEM(lookups, BF16),
            pltpu.VMEM(lookups, BF16),
            pltpu.VMEM((imps, table_count * width), BF16),
            pltpu.VMEM((table_count * width, imps), BF16),
            pltpu.VMEM(lookups, BF16),
            pltpu.VMEM(lookups, BF16),
            pltpu.VMEM(lookups, BF16),
            pltpu.VMEM((CHUNKS, 2, inner, outer, rows, piece), F32),
            pltpu.VMEM((CHUNKS, inner, outer, rows, piece), F32),
            pltpu.VMEM((CHUNKS, inner, outer, rows, piece), F32),
            pltpu.VMEM((CHUNKS, inner, outer, rows, piece), I16),
            pltpu.VMEM((CHUNKS, inner, 1, piece), F32),
            pltpu.VMEM((CHUNKS, inner - 1, outer, rows, piece), I16),
            pltpu.VMEM((CHUNKS, inner - 1, 1, piece), F32),
            pltpu.VMEM((CHUNKS, outer, rows, piece), F32),
            pltpu.VMEM((CHUNKS, outer, rows, piece), I16),
            pltpu.VMEM((CHUNKS, outer, 1, piece), F32),
            pltpu.VMEM((CHUNKS, outer - 1, rows, piece), I16),
            pltpu.VMEM((CHUNKS, outer - 1, 1, piece), F32),
            pltpu.VMEM((8, hid), F32),
            pltpu.VMEM((8, hid), F32),
            pltpu.VMEM((inner, 8, hid), F32),
            pltpu.VMEM((outer, 8, hid), F32),
            pltpu.VMEM((8, hid), F32),
            pltpu.VMEM((8, hid), F32),
            dma((table_count,)), dma((8,)), dma((2,)),
            dma((table_count,)), dma((table_count,)), dma((2,)), dma((table_count,)),
            dma((table_count,)), dma((table_count,)), dma((table_count,)),
            dma((3, CHUNKS)), dma((3, CHUNKS)),
            dma((4, CHUNKS)), dma((4, CHUNKS)), dma((4, CHUNKS)), dma((4, CHUNKS)),
            dma((3,)), dma((3,)),
        ],
        compiler_params=pltpu.CompilerParams(
            collective_id=1, has_side_effects=True, vmem_limit_bytes=44 * 1024 * 1024
        ),
    )(
        *(
            pltpu.with_memory_space_constraint(operand, pltpu.HBM)
            for operand in (
                tables, owner_ids, row_ids, session, relevance, logit_bias, w_hidden, bias_hidden,
                w_score,
            )
        )
    )
    params = hid * hid + 2 * hid
    emb_step, step_hidden, step_bias, step_score, loss = pl.pallas_call(
        functools.partial(write_body, params, SESS_DEV * owners * 2),
        out_shape=(
            jax.ShapeDtypeStruct((table_count, half_rows, width), F32),
            jax.ShapeDtypeStruct((hid, hid), F32),
            jax.ShapeDtypeStruct((1, hid), F32),
            jax.ShapeDtypeStruct((1, hid), F32),
            jax.ShapeDtypeStruct((1, 1), F32),
        ),
        in_specs=[vmem] * 4,
        out_specs=(hbm,) * 5,
        scratch_shapes=[
            pltpu.VMEM((hid, hid), F32), pltpu.VMEM((1, hid), F32), pltpu.VMEM((1, hid), F32),
            pltpu.VMEM((1, 1), F32), dma((table_count,)), dma((4,)),
        ],
        compiler_params=pltpu.CompilerParams(vmem_limit_bytes=8 * 1024 * 1024),
    )(emb_rows, codes, scales, small)
    return (emb_step, step_hidden, step_bias[0], step_score[0], loss[0, 0])


def solution(mesh):
    in_specs = (
        P(None, "table", None),
        P(("table", "dp"), None, None, None),
        P(("table", "dp"), None, None),
        P(("table", "dp"), None),
        P(("table", "dp"), None),
        P(("table", "dp"), None),
        P(),
        P(),
        P(),
    )
    out_specs = (P(None, ("table", "dp"), None), P(), P(), P(), P())
    return jax.shard_map(
        on_device, mesh=mesh, in_specs=in_specs, out_specs=out_specs, check_vma=False
    )
```

time: 79.7 us -> 54.3 us (0.68)
  Pallas kernels: 69.3 us -> 53.5 us
  local copies, waits for them, and re-layouts: 6.5 us -> 0 us
  other arithmetic: 2.62 us -> 0 us
    pallas_call x1, Pallas kernels: 66.3 us -> 51 us  [whole_kernel(): pl.pallas_call(functools.partial(whole_body, sizes), out_shape=(jax.Shape...]
    unnamed x9 -> x0, local copies, waits for them, and re-layouts: 5.46 us -> none
    reduce_sum x1 -> x0, other arithmetic: 1.23 us -> none  [on_device(): jnp.sum(slot_hot, axis=1)]
    another operation x2 -> x0, local copies, waits for them, and re-layouts: 0.85 us -> none  [whole_kernel(): jnp.stack([slot_of[table].astype(jnp.float32) for table in range(table_co...]
where the time goes in v2:
time: 54.3 us; the launch traced here: 54.1 us
  Pallas kernels  53.5 us (99%)
  between operations  0.64 us (1%)
    pallas_call x1, Pallas kernels, whole_kernel(): pl.pallas_call(functools.partial(whole_body, sizes), out_shape=(jax.Shape...  51 us
    pallas_call x1, Pallas kernels, whole_kernel(): pl.pallas_call(functools.partial(write_body, params, SESS_DEV * owners *...  2.43 us

profile of v2, /device:TPU:0, one launch (start us, length us, event | category | flops | bytes accessed | tf_op | source)
XLA Modules:
  0.0 54.1 jit_solution(9110724227815768063)
XLA Ops:
  0.6 51.0 %shard_map.128 = (f32[4,2048,128]{2,1,0:T(8,128)S(1)}, s16[2,2,4,4,16,256]{5,4,3,2,1,0:T(8,128)(2,1)S(1)}, f32[2,2,4,4,1,256]{5,4,3,2,1,0:T(1,128)S(1)}, f32[8,512]{1,0:T(8,128)S(1)}) custom-call(bf16[4,4096,128]{2,1,0:T(8,128)(2,1)} %tables_hbm.1, s32[4,1,256]{2,1,0:T(1,128)} %bitcast.7, s32[4,256]{1,0:T(4,128)} %bitcast.8, s32[1,256]{1,0:T(1,128)} %session_hbm.1, ...), custom_call_target="tpu_custom_call" | custom-call | tf_op jit(solution)/shard_map/pallas_call | solution.py:763
  51.7 2.4 %shard_map.129 = (f32[4,2048,128]{2,1,0:T(8,128)}, f32[512,512]{1,0:T(8,128)}, f32[1,512]{1,0:T(1,128)}, f32[1,512]{1,0:T(1,128)}, f32[1,1]{1,0:T(1,128)}) custom-call(f32[4,2048,128]{2,1,0:T(8,128)S(1)} %get-tuple-element.14.rows_hbm, s16[2,2,4,4,16,256]{5,4,3,2,1,0:T(8,128)(2,1)S(1)} %get-tuple-element.15.code_ref, ...), custom_call_target="tpu_custom_call" | custom-call | tf_op jit(solution)/shard_map/pallas_call | solution.py:841

commit v3 on v2

--- a/solution.py
+++ b/solution.py
@@ -206,6 +206,7 @@
     low, high = lax.rem(me, inner), me // inner
     other = (me, 1 - core)
     half = outer // 2
+    is_hub = (high >= half - 1) & (high <= half)
 
     barrier = pltpu.get_barrier_semaphore()
 
@@ -227,15 +228,11 @@
         pltpu.make_async_copy(src, dst, fetch_sem.at[at]) for at, (src, dst) in enumerate(sources)
     ]
 
-    def load(table):
-        return pltpu.make_async_copy(
-            tables_hbm.at[table], tables_ref.at[table], load_sem.at[table]
-        )
+    load = pltpu.make_async_copy(tables_hbm, tables_ref, load_sem.at[0])
 
     for fetch in fetches:
         fetch.start()
-    for table in range(tables):
-        load(table).start()
+    load.start()
 
     def remote(src, dst, send, recv, to):
         return pltpu.make_async_remote_copy(
@@ -243,7 +240,7 @@
             device_id_type=MESH,
         )
 
-    def to_peers(copy_to):
+    def to_peers(copy_to, far_too=True, near_too=True):
         def far(step, carry):
             plane = (1 - high // half) * half + step // inner
             copy_to(plane * inner + lax.rem(low + lax.rem(step, inner), inner)).start()
@@ -258,9 +255,11 @@
             copy_to(high * inner + lax.rem(low + step, inner)).start()
             return carry
 
-        lax.fori_loop(0, half * inner, far, 0)
-        lax.fori_loop(0, (half - 1) * inner, near, 0)
-        lax.fori_loop(1, inner, level, 0)
+        if far_too:
+            lax.fori_loop(0, half * inner, far, 0)
+        if near_too:
+            lax.fori_loop(0, (half - 1) * inner, near, 0)
+            lax.fori_loop(1, inner, level, 0)
 
     for fetch in fetches[:5]:
         fetch.wait()
@@ -342,11 +341,14 @@
     codes_mine = expand(ids_in)
     ids_cols[...] = columns_of(codes_mine)
 
-    def pick(table):
-        code = ids_cols[:, table * LANES : (table + 1) * LANES]
+    def pick(table, first, count):
+        code = ids_cols[
+            pl.ds(pl.multiple_of(first * capacity, capacity), count * capacity),
+            table * LANES : (table + 1) * LANES,
+        ]
         upper = code > half_rows
         key = jnp.where(upper, code - (half_rows + 1.0), code - 1.0).astype(jnp.int32).astype(I16)
-        both = jnp.zeros((slots, 2 * width), F32)
+        both = jnp.zeros((count * capacity, 2 * width), F32)
         depth = 256
         for at in range(0, half_rows, depth):
             rows = jnp.concatenate(
@@ -359,21 +361,34 @@
             both = both + jnp.dot(
                 lane_hits(key, at, depth // LANES), rows, preferred_element_type=F32
             )
-        served[table] = jnp.where(upper, both[:, width:], both[:, :width]).astype(BF16).reshape(
-            owners, capacity, width
+        served[table, pl.ds(first, count)] = (
+            jnp.where(upper, both[:, width:], both[:, :width])
+            .astype(BF16)
+            .reshape(count, capacity, width)
+        )
+
+    def serve(table, far_too, near_too):
+        to_peers(
+            lambda peer: remote(
+                served.at[table, peer], picked.at[table, me], serve_send.at[table],
+                serve_recv.at[table], (peer, core),
+            ),
+            far_too, near_too,
         )
 
     with jax.named_scope("pick"):
+        load.wait()
+        side = high // half
+        part = owners // 2
+        pick(0, (1 - side) * part, part)
+        serve(0, True, False)
+        pick(0, side * part, part)
+        serve(0, False, True)
+        for table in range(1, tables):
+            pick(table, 0, owners)
+            serve(table, True, True)
         for table in range(tables):
-            load(table).wait()
-            pick(table)
             picked[table, me] = served[table, me]
-            to_peers(
-                lambda peer, table=table: remote(
-                    served.at[table, peer], picked.at[table, me], serve_send.at[table],
-                    serve_recv.at[table], (peer, core),
-                )
-            )
 
     with jax.named_scope("prep"):
         for table in range(tables):
@@ -407,7 +422,20 @@
         codes_theirs = expand(ids_other)
         place_prep(codes_theirs, columns_of(codes_theirs), slots)
 
-    pre_act = jnp.broadcast_to(bias_ref[...], (imps, hid))
+    session = columns_ref[:, tables : tables + 1].astype(jnp.int32)
+    relevance = columns_ref[:, tables + 1 : tables + 2]
+
+    def of_session(values, reduce, fill):
+        found = [
+            reduce(jnp.where(session == at, values, fill), axis=0, keepdims=True)
+            for at in range(SESS_DEV)
+        ]
+        each = jnp.broadcast_to(found[-1], values.shape)
+        for at in range(SESS_DEV - 1):
+            each = jnp.where(session == at, found[at], each)
+        return found, each
+
+    target = relevance / of_session(relevance, jnp.sum, 0.0)[1]
     for table in range(tables):
         with jax.named_scope(f"rows_wait{table}"):
             remote(
@@ -423,28 +451,16 @@
         pre_act = jnp.dot(gathered[...], w_bf[...], preferred_element_type=F32) + bias_ref[...]
         logistic = 1.0 / (1.0 + jnp.exp(-pre_act))
         hidden = pre_act * logistic
-        session = columns_ref[:, tables : tables + 1].astype(jnp.int32)
-        relevance = columns_ref[:, tables + 1 : tables + 2]
         scores = jnp.sum(hidden * scorer_ref[...], axis=1, keepdims=True)
         scores = scores + columns_ref[:, tables + 2 : tables + 3]
-        member = iota((imps, LANES), 1) == session
-        highest = jnp.max(jnp.where(member, scores, -jnp.inf), axis=0, keepdims=True)
-        highest_each = jnp.sum(jnp.where(member, highest, 0.0), axis=1, keepdims=True)
-        shifted = scores - highest_each
+        shifted = scores - of_session(scores, jnp.max, -jnp.inf)[1]
         exponent = jnp.exp(shifted)
-        sums = jnp.sum(jnp.where(member, exponent, 0.0), axis=0, keepdims=True)
-        weights = jnp.sum(jnp.where(member, relevance, 0.0), axis=0, keepdims=True)
-        sum_each = jnp.sum(jnp.where(member, sums, 0.0), axis=1, keepdims=True)
-        weight_each = jnp.sum(jnp.where(member, weights, 0.0), axis=1, keepdims=True)
-        target = relevance / weight_each
-        real = iota((1, LANES), 1) < SESS_DEV
-        loss_sum = jnp.sum(jnp.log(jnp.where(real, sums, 1.0)), keepdims=True) - jnp.sum(
-            target * shifted, keepdims=True
-        )
+        sums, sum_each = of_session(exponent, jnp.sum, 0.0)
+        loss_sum = sum(jnp.log(value) for value in sums) - jnp.sum(target * shifted, keepdims=True)
         score_grad = exponent / sum_each - target
         pre_grad = score_grad * scorer_ref[...] * (logistic * (1.0 + pre_act * (1.0 - logistic)))
         pre_grad_bf = pre_grad.astype(BF16)
-    piece, rows = hid // CHUNKS, hid // (2 * owners)
+    piece, rows = hid // CHUNKS, hid // (4 * inner)
 
     def pair_up(chunk):
         return remote(
@@ -452,36 +468,43 @@
             pair_recv.at[0, chunk], other,
         )
 
-    with jax.named_scope("weight_grad"):
-        for chunk in range(CHUNKS):
-            dense_ref[chunk] = jnp.dot(
-                inputs_t[...], pre_grad_bf[:, chunk * piece : (chunk + 1) * piece],
-                preferred_element_type=F32,
-            ).reshape(dense_ref.shape[1:])
-            pair_up(chunk).start()
-        extra_ref[...] = jnp.zeros_like(extra_ref)
-        extra_ref[0:1, :] = jnp.sum(pre_grad, axis=0, keepdims=True)
-        extra_ref[1:2, :] = jnp.sum(score_grad * hidden, axis=0, keepdims=True)
-        extra_ref[2:3, :] = jnp.broadcast_to(loss_sum, (1, hid))
-        extra_up = remote(extra_ref, extra_other, extra_send.at[0], extra_recv.at[0], other)
-        extra_up.start()
-    with jax.named_scope("input_grad"):
-        input_grad = lax.dot_general(
-            pre_grad_bf, w_bf[...], (((1,), (1,)), ((), ())), preferred_element_type=F32
-        ).astype(BF16)
-
-    def send_grads(table):
-        out_ref[table] = jnp.dot(
-            hot_rows[table], input_grad[:, table * width : (table + 1) * width],
+    extra_up = remote(extra_ref, extra_other, extra_send.at[0], extra_recv.at[0], other)
+
+    def weight_step(chunk):
+        dense_ref[chunk] = jnp.dot(
+            inputs_t[...], pre_grad_bf[:, chunk * piece : (chunk + 1) * piece],
             preferred_element_type=F32,
-        ).astype(BF16).reshape(owners, capacity, width)
-        grads[table, me] = out_ref[table, me]
+        ).reshape(dense_ref.shape[1:])
+        pair_up(chunk).start()
+        if chunk == CHUNKS - 1:
+            extra_ref[...] = jnp.zeros_like(extra_ref)
+            extra_ref[0:1, :] = jnp.sum(pre_grad, axis=0, keepdims=True)
+            extra_ref[1:2, :] = jnp.sum(score_grad * hidden, axis=0, keepdims=True)
+            extra_ref[2:3, :] = jnp.broadcast_to(loss_sum, (1, hid))
+            extra_up.start()
+
+    def give(table, far_too, near_too):
         to_peers(
             lambda peer: remote(
                 out_ref.at[table, peer], grads.at[table, me], grad_send.at[table],
                 grad_recv.at[table], (peer, core),
-            )
-        )
+            ),
+            far_too, near_too,
+        )
+
+    def near_step(table):
+        give(table, False, True)
+
+    def send_grads(table):
+        input_grad = lax.dot_general(
+            pre_grad_bf, w_bf[table * width : (table + 1) * width, :], (((1,), (1,)), ((), ())),
+            preferred_element_type=F32,
+        ).astype(BF16)
+        out_ref[table] = jnp.dot(
+            hot_rows[table], input_grad, preferred_element_type=F32
+        ).astype(BF16).reshape(owners, capacity, width)
+        grads[table, me] = out_ref[table, me]
+        give(table, True, False)
 
     def swap(table):
         return remote(
@@ -528,10 +551,12 @@
             to = lax.rem(low + step, inner)
             remote(src_of(to), dst_of(step - 1), send, recv, (high * inner + to, core)).start()
 
-    def to_column(src_of, dst_of, send, recv):
+    def to_column(src, dst, send, recv):
         for step in range(1, outer):
             to = lax.rem(high + step, outer)
-            remote(src_of(to), dst_of(step - 1), send, recv, (to * inner + low, core)).start()
+            remote(src, dst, send, recv, (to * inner + low, core)).start()
+
+    columns = ((column_s, from_column_s), (column_q, from_column_q))
 
     def await_all(src, dst, send, recv):
         remote(src, dst, send, recv, other).wait()
@@ -551,31 +576,50 @@
             )
 
     def column_sum(chunk):
-        for at, (src, dst) in enumerate(((column_s, from_column_s), (column_q, from_column_q))):
-            to_column(
-                lambda to: src.at[chunk, to], lambda slot: dst.at[chunk, slot],
-                column_send.at[at, chunk], column_recv.at[at, chunk],
-            )
+        for hub in range(2):
+
+            @pl.when(high != half - 1 + hub)
+            def _():
+                for at, (src, dst) in enumerate(columns):
+                    remote(
+                        src.at[chunk, hub], dst.at[chunk, high], column_send.at[at, chunk],
+                        column_recv.at[at, chunk], ((half - 1 + hub) * inner + low, core),
+                    ).start()
 
     def column_summed(chunk):
-        for at, (src, dst) in enumerate(((column_s, from_column_s), (column_q, from_column_q))):
-            await_all(
-                src.at[chunk, pl.ds(0, outer - 1)], dst.at[chunk], column_send.at[at, chunk],
-                column_recv.at[at, chunk],
-            )
+        for at, (src, dst) in enumerate(columns):
+            sems = column_send.at[at, chunk], column_recv.at[at, chunk], other
+
+            @pl.when(is_hub)
+            def _():
+                remote(src.at[chunk, 0], dst.at[chunk, 0], *sems).wait_send()
+                some = dst.at[chunk, pl.ds(0, outer - 1)]
+                remote(some, some, *sems).wait_recv()
+
+            @pl.when(jnp.logical_not(is_hub))
+            def _():
+                remote(src.at[chunk], src.at[chunk], *sems).wait_send()
 
     def column_share(chunk):
         for at, part in enumerate((share_s, share_q)):
-            mine = part.at[chunk, core, low, high]
-            to_column(
-                lambda to: mine, lambda slot: mine, column_send.at[2 + at, chunk],
-                column_recv.at[2 + at, chunk],
-            )
+            mine = part.at[chunk, core, low, high - (half - 1)]
+            to_column(mine, mine, column_send.at[2 + at, chunk], column_recv.at[2 + at, chunk])
 
     def column_shared(chunk):
         for at, part in enumerate((share_s, share_q)):
-            some = part.at[chunk, core, low, pl.ds(0, outer - 1)]
-            await_all(some, some, column_send.at[2 + at, chunk], column_recv.at[2 + at, chunk])
+            sems = column_send.at[2 + at, chunk], column_recv.at[2 + at, chunk], other
+
+            @pl.when(is_hub)
+            def _():
+                some = columns[at][1].at[chunk, pl.ds(0, outer - 1)]
+                remote(some, some, *sems).wait_send()
+                one = part.at[chunk, core, low, 0]
+                remote(one, one, *sems).wait_recv()
+
+            @pl.when(jnp.logical_not(is_hub))
+            def _():
+                both = part.at[chunk, core, low]
+                remote(both, both, *sems).wait_recv()
 
     def plane_share(chunk):
         for at, part in enumerate((share_s, share_q)):
@@ -621,8 +665,8 @@
         for to in range(inner):
             values = dense_ref[chunk, core, to] + from_other[chunk, to]
             sum_pair[chunk, to] = values
-            code, plane_s[chunk, to] = coded(values.reshape(outer * rows, piece))
-            plane_q[chunk, to] = code.reshape(outer, rows, piece)
+            code, plane_s[chunk, to] = coded(values.reshape(2 * rows, piece))
+            plane_q[chunk, to] = code.reshape(2, rows, piece)
         plane_sum(chunk)
         if chunk == CHUNKS - 1:
             extra_up.wait()
@@ -635,12 +679,12 @@
 
     def plane_step(chunk):
         plane_summed(chunk)
-        part = sum_pair[chunk, low].reshape(outer * rows, piece)
+        part = sum_pair[chunk, low].reshape(2 * rows, piece)
         for slot in range(inner - 1):
             part = part + decoded(
-                from_plane_q[chunk, slot].reshape(outer * rows, piece), from_plane_s[chunk, slot]
+                from_plane_q[chunk, slot].reshape(2 * rows, piece), from_plane_s[chunk, slot]
             )
-        for to in range(outer):
+        for to in range(2):
             values = part[to * rows : (to + 1) * rows]
             sum_plane[chunk, to] = values
             column_q[chunk, to], column_s[chunk, to] = coded(values)
@@ -653,20 +697,23 @@
                 part = part + extra_plane[slot]
             extra_sum[...] = part
             extra_column[high] = part
-            to_column(
-                lambda to: extra_sum, lambda slot: extra_column.at[high], extra_send.at[2],
-                extra_recv.at[2],
-            )
+            to_column(extra_sum, extra_column.at[high], extra_send.at[2], extra_recv.at[2])
 
     def column_step(chunk):
         column_summed(chunk)
-        part = sum_plane[chunk, high]
-        for slot in range(outer - 1):
-            part = part + decoded(from_column_q[chunk, slot], from_column_s[chunk, slot])
-        code, scale = coded(part)
-        share_q[chunk, core, low, high] = code
-        share_s[chunk, core, low, high] = scale
-        column_share(chunk)
+
+        @pl.when(is_hub)
+        def _():
+            hub = high - (half - 1)
+            part = sum_plane[chunk, hub]
+            for step in range(1, outer):
+                at = lax.rem(high + step, outer)
+                part = part + decoded(from_column_q[chunk, at], from_column_s[chunk, at])
+            code, scale = coded(part)
+            share_q[chunk, core, low, hub] = code
+            share_s[chunk, core, low, hub] = scale
+            column_share(chunk)
+
         if chunk == CHUNKS - 1:
             some = extra_column.at[pl.ds(0, outer - 1)]
             await_all(some, some, extra_send.at[2], extra_recv.at[2])
@@ -687,7 +734,7 @@
         finish(pair_down(chunk))
 
     steps = {
-        "send": send_grads, "pair": pair_step, "plane": plane_step, "column": column_step,
+        "weight": weight_step, "far": send_grads, "near": near_step, "pair": pair_step, "plane": plane_step, "column": column_step,
         "share": share_step, "down": down_step, "last": last_step, "arrive": arrive, "place": place,
     }
     for word in ORDER:
@@ -696,9 +743,10 @@
 
 
 ORDER = (
-    "send0", "pair0", "pair1", "send1", "send2", "plane0", "send3", "plane1", "arrive0",
-    "place0", "column0", "arrive1", "place1", "column1", "arrive2", "share0", "share1",
-    "place2", "arrive3", "down0", "down1", "place3", "last0", "last1",
+    "far0", "weight0", "weight1", "far1", "pair0", "pair1", "far2", "plane0", "near0",
+    "plane1", "near1", "far3", "near2", "near3", "column0", "arrive0", "column1", "place0",
+    "share0", "arrive1", "share1", "place1", "arrive2", "down0", "down1", "arrive3", "place2",
+    "place3", "last0", "last1",
 )
 
 
@@ -753,7 +801,7 @@
     while inner * inner < owners:
         inner *= 2
     outer = owners // inner
-    rows = hid // (2 * owners)
+    rows = hid // (4 * inner)
     piece = hid // CHUNKS
     sizes = (table_count, owners, capacity, width, half_rows, inner, outer, hid)
     dma = pltpu.SemaphoreType.DMA
@@ -764,9 +812,9 @@
         functools.partial(whole_body, sizes),
         out_shape=(
             jax.ShapeDtypeStruct((table_count, half_rows, width), F32),
-            jax.ShapeDtypeStruct((CHUNKS, 2, inner, outer, rows, piece), I16),
-            jax.ShapeDtypeStruct((CHUNKS, 2, inner, outer, 1, piece), F32),
-            jax.ShapeDtypeStruct((8, hid), F32),
+            jax.ShapeDtypeStruct((CHUNKS, 2, inner, 2, rows, piece), I16),
+            jax.ShapeDtypeStruct((CHUNKS, 2, inner, 2, 1, piece), F32),
+            jax.ShapeDtypeStruct((4, hid), F32),
         ),
         in_specs=[hbm] * 9,
         out_specs=(vmem, vmem, vmem, vmem),
@@ -800,25 +848,25 @@
             pltpu.VMEM(lookups, BF16),
             pltpu.VMEM(lookups, BF16),
             pltpu.VMEM(lookups, BF16),
-            pltpu.VMEM((CHUNKS, 2, inner, outer, rows, piece), F32),
-            pltpu.VMEM((CHUNKS, inner, outer, rows, piece), F32),
-            pltpu.VMEM((CHUNKS, inner, outer, rows, piece), F32),
-            pltpu.VMEM((CHUNKS, inner, outer, rows, piece), I16),
+            pltpu.VMEM((CHUNKS, 2, inner, 2, rows, piece), F32),
+            pltpu.VMEM((CHUNKS, inner, 2, rows, piece), F32),
+            pltpu.VMEM((CHUNKS, inner, 2, rows, piece), F32),
+            pltpu.VMEM((CHUNKS, inner, 2, rows, piece), I16),
             pltpu.VMEM((CHUNKS, inner, 1, piece), F32),
-            pltpu.VMEM((CHUNKS, inner - 1, outer, rows, piece), I16),
+            pltpu.VMEM((CHUNKS, inner - 1, 2, rows, piece), I16),
             pltpu.VMEM((CHUNKS, inner - 1, 1, piece), F32),
-            pltpu.VMEM((CHUNKS, outer, rows, piece), F32),
+            pltpu.VMEM((CHUNKS, 2, rows, piece), F32),
+            pltpu.VMEM((CHUNKS, 2, rows, piece), I16),
+            pltpu.VMEM((CHUNKS, 2, 1, piece), F32),
             pltpu.VMEM((CHUNKS, outer, rows, piece), I16),
             pltpu.VMEM((CHUNKS, outer, 1, piece), F32),
-            pltpu.VMEM((CHUNKS, outer - 1, rows, piece), I16),
-            pltpu.VMEM((CHUNKS, outer - 1, 1, piece), F32),
-            pltpu.VMEM((8, hid), F32),
-            pltpu.VMEM((8, hid), F32),
-            pltpu.VMEM((inner, 8, hid), F32),
-            pltpu.VMEM((outer, 8, hid), F32),
-            pltpu.VMEM((8, hid), F32),
-            pltpu.VMEM((8, hid), F32),
-            dma((table_count,)), dma((8,)), dma((2,)),
+            pltpu.VMEM((4, hid), F32),
+            pltpu.VMEM((4, hid), F32),
+            pltpu.VMEM((inner, 4, hid), F32),
+            pltpu.VMEM((outer, 4, hid), F32),
+            pltpu.VMEM((4, hid), F32),
+            pltpu.VMEM((4, hid), F32),
+            dma((1,)), dma((8,)), dma((2,)),
             dma((table_count,)), dma((table_count,)), dma((2,)), dma((table_count,)),
             dma((table_count,)), dma((table_count,)), dma((table_count,)),
             dma((3, CHUNKS)), dma((3, CHUNKS)),

time: 54.3 us -> 52.5 us (0.967)
  Pallas kernels: 53.5 us -> 51.7 us
    pallas_call x1, Pallas kernels: 51 us -> 49.3 us  [whole_kernel(): pl.pallas_call(functools.partial(whole_body, sizes), out_shape=(jax.Shape...]
where the time goes in v3:
time: 52.5 us; the launch traced here: 52.3 us
  Pallas kernels  51.7 us (98%)
  between operations  0.64 us (1%)
    pallas_call x1, Pallas kernels, whole_kernel(): pl.pallas_call(functools.partial(whole_body, sizes), out_shape=(jax.Shape...  49.3 us
    pallas_call x1, Pallas kernels, whole_kernel(): pl.pallas_call(functools.partial(write_body, params, SESS_DEV * owners *...  2.43 us

profile of v3, /device:TPU:0, one launch (start us, length us, event | category | flops | bytes accessed | tf_op | source)
XLA Modules:
  0.0 52.3 jit_solution(12163060154448008131)
XLA Ops:
  0.6 49.3 %shard_map.128 = (f32[4,2048,128]{2,1,0:T(8,128)S(1)}, s16[2,2,4,2,32,256]{5,4,3,2,1,0:T(8,128)(2,1)S(1)}, f32[2,2,4,2,1,256]{5,4,3,2,1,0:T(1,128)S(1)}, f32[4,512]{1,0:T(4,128)S(1)}) custom-call(bf16[4,4096,128]{2,1,0:T(8,128)(2,1)} %tables_hbm.1, s32[4,1,256]{2,1,0:T(1,128)} %bitcast.7, s32[4,256]{1,0:T(4,128)} %bitcast.8, s32[1,256]{1,0:T(1,128)} %session_hbm.1, ...), custom_call_target="tpu_custom_call" | custom-call | tf_op jit(solution)/shard_map/pallas_call | solution.py:811
  49.9 2.4 %shard_map.129 = (f32[4,2048,128]{2,1,0:T(8,128)}, f32[512,512]{1,0:T(8,128)}, f32[1,512]{1,0:T(1,128)}, f32[1,512]{1,0:T(1,128)}, f32[1,1]{1,0:T(1,128)}) custom-call(f32[4,2048,128]{2,1,0:T(8,128)S(1)} %get-tuple-element.14.rows_hbm, s16[2,2,4,2,32,256]{5,4,3,2,1,0:T(8,128)(2,1)S(1)} %get-tuple-element.15.code_ref, ...), custom_call_target="tpu_custom_call" | custom-call | tf_op jit(solution)/shard_map/pallas_call | solution.py:889

commit v4 on v3

--- a/solution.py
+++ b/solution.py
@@ -242,7 +242,8 @@
 
     def to_peers(copy_to, far_too=True, near_too=True):
         def far(step, carry):
-            plane = (1 - high // half) * half + step // inner
+            up = (1 - high // half) * (half - 1 - 2 * (step // inner))
+            plane = (1 - high // half) * half + step // inner + up
             copy_to(plane * inner + lax.rem(low + lax.rem(step, inner), inner)).start()
             return carry
 
@@ -743,10 +744,10 @@
 
 
 ORDER = (
-    "far0", "weight0", "weight1", "far1", "pair0", "pair1", "far2", "plane0", "near0",
-    "plane1", "near1", "far3", "near2", "near3", "column0", "arrive0", "column1", "place0",
-    "share0", "arrive1", "share1", "place1", "arrive2", "down0", "down1", "arrive3", "place2",
-    "place3", "last0", "last1",
+    "far0", "weight0", "weight1", "far1", "pair0", "pair1", "far2", "plane0", "near0", "near1",
+    "plane1", "far3", "near2", "near3", "column0", "arrive0", "column1", "arrive1", "place0",
+    "share0", "arrive2", "share1", "place1", "arrive3", "down0", "place2", "down1", "place3",
+    "last0", "last1",
 )
 
 

time: 52.5 us -> 51.6 us (0.983)
  Pallas kernels: 51.7 us -> 50.7 us
    pallas_call x1, Pallas kernels: 49.3 us -> 48.2 us  [whole_kernel(): pl.pallas_call(functools.partial(whole_body, sizes), out_shape=(jax.Shape...]
where the time goes in v4:
time: 51.6 us; the launch traced here: 51.5 us
  Pallas kernels  50.7 us (98%)
  between operations  0.8 us (2%)
    pallas_call x1, Pallas kernels, whole_kernel(): pl.pallas_call(functools.partial(whole_body, sizes), out_shape=(jax.Shape...  48.2 us
    pallas_call x1, Pallas kernels, whole_kernel(): pl.pallas_call(functools.partial(write_body, params, SESS_DEV * owners *...  2.43 us

profile of v4, /device:TPU:0, one launch (start us, length us, event | category | flops | bytes accessed | tf_op | source)
XLA Modules:
  0.0 51.5 jit_solution(14085609444272625712)
XLA Ops:
  0.6 48.2 %shard_map.128 = (f32[4,2048,128]{2,1,0:T(8,128)S(1)}, s16[2,2,4,2,32,256]{5,4,3,2,1,0:T(8,128)(2,1)S(1)}, f32[2,2,4,2,1,256]{5,4,3,2,1,0:T(1,128)S(1)}, f32[4,512]{1,0:T(4,128)S(1)}) custom-call(bf16[4,4096,128]{2,1,0:T(8,128)(2,1)} %tables_hbm.1, s32[4,1,256]{2,1,0:T(1,128)} %bitcast.7, s32[4,256]{1,0:T(4,128)} %bitcast.8, s32[1,256]{1,0:T(1,128)} %session_hbm.1, ...), custom_call_target="tpu_custom_call" | custom-call | tf_op jit(solution)/shard_map/pallas_call | solution.py:812
  48.9 2.4 %shard_map.129 = (f32[4,2048,128]{2,1,0:T(8,128)}, f32[512,512]{1,0:T(8,128)}, f32[1,512]{1,0:T(1,128)}, f32[1,512]{1,0:T(1,128)}, f32[1,1]{1,0:T(1,128)}) custom-call(f32[4,2048,128]{2,1,0:T(8,128)S(1)} %get-tuple-element.14.rows_hbm, s16[2,2,4,2,32,256]{5,4,3,2,1,0:T(8,128)(2,1)S(1)} %get-tuple-element.15.code_ref, ...), custom_call_target="tpu_custom_call" | custom-call | tf_op jit(solution)/shard_map/pallas_call | solution.py:890
